TPU v7x, 32 devices: a whole 2x2x4 slice. The times are simulated.
32 devices in a mesh: vocab: 16 (over z, y, x), tok: 2 (over core).
Axes of the slice: x: 2, y: 2, z: 4, core: 2. Of those that a mesh axis runs over, the one named last changes fastest.
Arguments:
- hidden: bfloat16 [384, 3584], P('vocab', 'tok'), may hold values from -6 to 6
- embedding: bfloat16 [131072, 3584], P('vocab', 'tok'), may hold values from -0.3125 to 0.3125
- embed_cotangent: bfloat16 [384, 3584], P('vocab', 'tok'), may hold values from -0.119628906 to 0.119628906
- input_ids: int32 [384], P('vocab'), may hold values from 0 to 131071
- target_ids: int32 [384], P('vocab'), may hold values from 0 to 131071
Outputs:
- embedding_grad: bfloat16 [131072, 3584], P('vocab', 'tok')
- hidden_grad: bfloat16 [384, 3584], P('vocab', 'tok')
- token_loss: float32 [384], P('vocab')
All inputs are finite; a program needn't handle non-finite values.
Results may differ from a plain program's by a relative error of at most 0.0037.
Values may be sent and summed in bfloat16 or wider, within the bound.
No kernel may reach another device: no remote copies, remote signals or barrier semaphores. Data moves between devices by JAX's collectives and lax.ppermute only.
A program may use at most 192 MiB of HBM per device.

v0:
```python
import math

import jax
import jax.numpy as jnp
from jax import lax
from jax.sharding import PartitionSpec as P

D = 3584


softcap = 30.0
zloss_weight = 0.001


def column_stats(logits, first_column, targets):
    capped = softcap * jnp.tanh(logits / softcap)
    exponent = jnp.exp(capped - softcap)
    columns = first_column + jnp.arange(logits.shape[1], dtype=jnp.int32)
    target_hot = targets[:, None] == columns[None, :]
    local_total = jnp.sum(exponent, axis=1)
    local_target = jnp.sum(jnp.where(target_hot, capped, jnp.zeros_like(capped)), axis=1)
    return (capped, exponent, target_hot, local_total, local_target)


def column_grad(capped, exponent, target_hot, row_total, log_total):
    factor = 1.0 + 2.0 * zloss_weight * log_total
    capped_grad = factor[:, None] * exponent / row_total[:, None] - target_hot.astype(jnp.float32)
    ratio = capped / softcap
    return (capped_grad * (1.0 - ratio * ratio)).astype(jnp.bfloat16)


def local(hidden, embedding, embed_cotangent, input_ids, target_ids):
    gathered, cotangent = (
        lax.all_gather(hidden, "vocab", axis=0, tiled=True),
        lax.all_gather(embed_cotangent, "vocab", axis=0, tiled=True),
    )
    input_all, target_all = (
        lax.all_gather(input_ids, "vocab", axis=0, tiled=True),
        lax.all_gather(target_ids, "vocab", axis=0, tiled=True),
    )
    rows_here = embedding.shape[0]
    partial_value = lax.dot_general(
        gathered, embedding, (((1,), (1,)), ((), ())), preferred_element_type=jnp.float32
    )
    first_row = lax.axis_index("vocab") * rows_here
    logits = lax.psum(partial_value, "tok")
    capped, exponent, target_hot, local_total, local_target = column_stats(
        logits, first_row, target_all
    )
    row_total, target_logit = lax.psum((local_total, local_target), "vocab")
    log_total = softcap + jnp.log(row_total)
    logit_grad = column_grad(capped, exponent, target_hot, row_total, log_total)
    loss_all = log_total - target_logit + zloss_weight * log_total * log_total
    local_count = input_ids.shape[0]
    token_loss = lax.dynamic_slice_in_dim(
        loss_all, lax.axis_index("vocab") * local_count, local_count, 0
    )
    hidden_grad = lax.psum_scatter(
        jnp.dot(logit_grad, embedding, preferred_element_type=jnp.float32),
        "vocab",
        scatter_dimension=0,
        tiled=True,
    ).astype(jnp.bfloat16)
    columns = first_row + jnp.arange(rows_here, dtype=jnp.int32)
    input_hot = (input_all[:, None] == columns[None, :]).astype(jnp.bfloat16)
    head_grad = lax.dot_general(
        logit_grad, gathered, (((0,), (0,)), ((), ())), preferred_element_type=jnp.float32
    )
    inject = lax.dot_general(
        input_hot, cotangent, (((0,), (0,)), ((), ())), preferred_element_type=jnp.float32
    )
    embed_scale = math.sqrt(D)
    embedding_grad = (head_grad + embed_scale * inject).astype(jnp.bfloat16)
    return (embedding_grad, hidden_grad, token_loss)


def solution(mesh):
    return jax.shard_map(
        local,
        mesh=mesh,
        in_specs=(P("vocab", "tok"), P("vocab", "tok"), P("vocab", "tok"), P("vocab"), P("vocab")),
        out_specs=(P("vocab", "tok"), P("vocab", "tok"), P("vocab")),
        check_vma=False,
    )
```

profile of v0, /device:TPU:0, one launch (start us, length us, event | category | flops | bytes accessed | tf_op | source)
XLA Modules:
  0.0 354.2 jit_solution(15666248329672211899)
XLA Ops:
  7.2 0.0 all-gather.3.cloned.1.call-start
  7.2 0.7 all-gather.3.cloned.1.call-update
  7.9 0.0 all-reduce.6.cloned.1.call-start
  7.9 62.5 %all-gather.3.cloned.1.call-done = bf16[384,1792]{1,0:T(8,128)(2,1)} async-done(((bf16[24,1792]{1,0:T(8,128)(2,1)}), bf16[384,1792]{1,0:T(8,128)(2,1)}) %all-gather.3.cloned.1.call-update) | async-done | bytes 1376272 | tf_op jit(solution)/shard_map/all_gather | solution.py:34
  70.4 19.6 %fusion.13 = f32[384,8192]{1,0:T(8,128)} fusion(bf16[384,1792]{1,0:T(8,128)(2,1)} %all-gather.3.cloned.1.call-done, bf16[8192,1792]{1,0:T(8,128)(2,1)} %param.6), kind=kOutput, calls=%fused_computation.20 | convolution fusion | flops 11274289152 | bytes 43319296 | tf_op jit(solution)/shard_map/dot_general | solution.py:42
  90.1 0.0 all-reduce.6.cloned.1.call-update
  90.1 0.0 all-gather.5.cloned.1.call-start
  90.1 0.7 all-gather.5.cloned.1.call-update
  90.8 0.0 reduce-scatter.2.cloned.1.call-start
  90.9 0.0 copy-done.3
  90.9 0.6 dynamic-slice
  92.2 0.2 dynamic-update-slice
  92.4 0.2 dynamic-update-slice.1
  92.6 13.3 %all-reduce.2 = (s32[384]{0:T(512)S(1)}, s32[384]{0:T(512)S(1)}) all-reduce(s32[384]{0:T(512)S(1)} %dynamic-update-slice, s32[384]{0:T(512)S(1)} %dynamic-update-slice.1), channel_id=1, replica_groups=mesh['vocab'=16,'tok'=2] {'vocab'}, use_global_device_ids=true, to_apply=%add | all-reduce | flops 768 | bytes 6144
  105.9 33.3 %all-reduce.6.cloned.1.call-done = f32[384,8192]{1,0:T(8,128)} async-done(((f32[384,8192]{1,0:T(8,128)}), f32[384,8192]{1,0:T(8,128)}) %all-reduce.6.cloned.1.call-update) | async-done | bytes 12582928 | tf_op jit(solution)/shard_map/psum | solution.py:46
  139.2 8.7 %fusion.3 = (f32[384]{0:T(512)S(1)}, f32[384]{0:T(512)S(1)}) fusion(f32[384,8192]{1,0:T(8,128)} %all-reduce.6.cloned.1.call-done, s32[8192]{0:T(1024)S(1)} %iota_add_fusion, s32[384]{0:T(512)S(1)} %get-tuple-element.5), kind=kLoop, calls=%fused_computation.6 | loop fusion | flops 22019328 | bytes 12620288 | tf_op jit(solution)/shard_map/reduce_sum | solution.py:21
  147.9 42.4 %all-reduce.3 = (f32[384]{0:T(512)S(1)}, f32[384]{0:T(512)S(1)}) all-reduce(f32[384]{0:T(512)S(1)} %get-tuple-element.4, f32[384]{0:T(512)S(1)} %get-tuple-element.3), channel_id=1, replica_groups=mesh['vocab'=16,'tok'=2] {'vocab'}, use_global_device_ids=true, to_apply=%region_2.3 | all-reduce | flops 768 | bytes 6144 | tf_op jit(solution)/shard_map/psum | solution.py:50
  190.3 28.5 %fusion.9 = f32[384,1792]{1,0:T(8,128)} fusion(bf16[8192,1792]{1,0:T(8,128)(2,1)} %param.6, f32[384,8192]{1,0:T(8,128)} %all-reduce.6.cloned.1.call-done, s32[8192]{0:T(1024)S(1)} %iota_add_fusion, f32[384]{0:T(512)S(1)} %get-tuple-element.7, f32[384]{0:T(512)S(1)} %get-tuple-element.10, s32[384]{0:T(512)S(1)} %get-tuple-element.5), kind=kOutput, calls=%fused_computation.18 | convolution fusion | flops 11312037888 | bytes 44732928 | tf_op jit(solution)/shard_map/dot_general | solution.py:59
  218.9 0.0 reduce-scatter.2.cloned.1.call-update
  218.9 30.8 %fusion.11 = f32[8192,1792]{1,0:T(8,128)} fusion(bf16[384,1792]{1,0:T(8,128)(2,1)S(1)} %copy-done, f32[384,8192]{1,0:T(8,128)} %all-reduce.6.cloned.1.call-done, s32[8192]{0:T(1024)S(1)} %iota_add_fusion, f32[384]{0:T(512)S(1)} %get-tuple-element.7, f32[384]{0:T(512)S(1)} %get-tuple-element.10, s32[384]{0:T(512)S(1)} %get-tuple-element.5), kind=kOutput, calls=%fused_computation.19 | convolution fusion | flops 11312037888 | bytes 72716800 | tf_op jit(solution)/shard_map/dot_general | solution.py:66
  249.7 0.6 dynamic_slice.3
  250.3 34.7 %add_convert_fusion = bf16[8192,1792]{1,0:T(8,128)(2,1)} fusion(f32[8192,1792]{1,0:T(8,128)} %fusion.11, bf16[384,1792]{1,0:T(8,128)(2,1)} %all-gather.5.cloned.1.call-done, s32[8192]{0:T(1024)S(1)} %iota_add_fusion, s32[384]{0:T(512)S(1)} %get-tuple-element.6), kind=kOutput, calls=%fused_computation | convolution fusion | flops 11321475072 | bytes 89490944 | tf_op jit(solution)/shard_map/dot_general | solution.py:69
  285.0 61.1 %reduce-scatter.2.cloned.1.call-done = f32[24,1792]{1,0:T(8,128)} async-done(((f32[384,1792]{1,0:T(8,128)}), f32[24,1792]{1,0:T(8,128)}) %reduce-scatter.2.cloned.1.call-update) | async-done | bytes 172048 | tf_op jit(solution)/shard_map/reduce_scatter | solution.py:58
  346.1 1.6 convert_element_type.16
  (12 shorter events, 0.0 us)
Async XLA Ops:
  7.2 63.3 %all-gather.3.cloned.1.call-start = ((), (), s32[]{:S(2)}) async-start(), calls=%async_computation.1 | async-start | bytes 1462272 | tf_op jit(solution)/shard_map/all_gather | solution.py:34
  7.9 131.3 %all-reduce.6.cloned.1.call-start = ((), (), s32[]{:S(2)}) async-start(), calls=%async_computation.2 | async-start | bytes 25165824 | tf_op jit(solution)/shard_map/psum | solution.py:46
  90.0 0.8 copy-start.3
  90.0 2.1 copy-start.1
  90.1 2.4 copy-start.2
  90.1 160.2 %all-gather.5.cloned.1.call-start = ((), (), s32[]{:S(2)}) async-start(), calls=%async_computation.3 | async-start | bytes 1462272 | tf_op jit(solution)/shard_map/all_gather | solution.py:35
  90.8 255.3 %reduce-scatter.2.cloned.1.call-start = ((), (), s32[]{:S(2)}) async-start(), calls=%async_computation.4 | async-start | bytes 2924544 | tf_op jit(solution)/shard_map/reduce_scatter | solution.py:58
  190.3 28.6 %copy-start = (bf16[384,1792]{1,0:T(8,128)(2,1)S(1)}, bf16[384,1792]{1,0:T(8,128)(2,1)}, u32[]{:S(2)}) copy-start(bf16[384,1792]{1,0:T(8,128)(2,1)} %all-gather.3.cloned.1.call-done) | copy-start | bytes 4128772
Sparse Core Ops, SparseCore 0:
  10.8 59.6 all-gather.2
  90.2 48.9 all-reduce.5
  142.0 58.2 all-gather.4
  219.0 127.0 reduce-scatter.1
where the time goes:
time: 355 us; the launch traced here: 354 us
  waiting for transfers between devices  158 us (45%)
  matrix products  114 us (32%)
  blocking collectives  55.7 us (16%)
  between operations  14.5 us (4%)
  other arithmetic  10.2 us (3%)
    all_gather x1, waiting for transfers between devices, local(): lax.all_gather(hidden, 'vocab', axis=0, tiled=True)  62.5 us
    reduce_scatter x1, waiting for transfers between devices, local(): lax.psum_scatter(jnp.dot(logit_grad, embedding, preferred_element_type=jn...  61.1 us
    psum x1, blocking collectives, local(): row_total, target_logit = lax.psum((local_total, local_target), 'vocab')  42.4 us
    dot_general x1, matrix products, local(): lax.dot_general(input_hot, cotangent, (((0,), (0,)), ((), ())), preferred...  34.7 us
    psum x1, waiting for transfers between devices, local(): logits = lax.psum(partial_value, 'tok')  33.3 us
    dot_general x1, matrix products, local(): lax.dot_general(logit_grad, gathered, (((0,), (0,)), ((), ())), preferred...  30.8 us
    dot_general x1, matrix products, local(): jnp.dot(logit_grad, embedding, preferred_element_type=jnp.float32)  28.5 us
    dot_general x1, matrix products, local(): lax.dot_general(gathered, embedding, (((1,), (1,)), ((), ())), preferred_...  19.6 us
  transfers between devices with their start and end apart: 4, of which 3 were waited for; matrix products, arithmetic and copies ran while one was open for 29% of the time, Pallas kernels for 0%

commit v1 on v0

v1 whole, which is shorter than its diff:
```python
import functools
import math

import jax
import jax.numpy as jnp
from jax import lax
from jax.experimental import pallas as pl
from jax.experimental.pallas import tpu as pltpu
from jax.sharding import PartitionSpec as P


softcap = 30.0
zloss_weight = 0.001
f32 = jnp.float32
bf16 = jnp.bfloat16


def column_stats(logits, first_column, targets):
    capped = softcap * jnp.tanh(logits / softcap)
    exponent = jnp.exp(capped - softcap)
    columns = first_column + jnp.arange(logits.shape[1], dtype=jnp.int32)
    target_hot = targets[:, None] == columns[None, :]
    local_total = jnp.sum(exponent, axis=1)
    local_target = jnp.sum(jnp.where(target_hot, capped, jnp.zeros_like(capped)), axis=1)
    return (capped, exponent, target_hot, local_total, local_target)


def column_grad(capped, exponent, target_hot, row_total, log_total):
    factor = 1.0 + 2.0 * zloss_weight * log_total
    capped_grad = factor[:, None] * exponent / row_total[:, None] - target_hot.astype(f32)
    ratio = capped / softcap
    return (capped_grad * (1.0 - ratio * ratio)).astype(bf16)


def plain(hidden, embedding, embed_cotangent, input_ids, target_ids, tok_count):
    gather = functools.partial(lax.all_gather, axis_name="vocab", axis=0, tiled=True)
    gathered, cotangent = gather(hidden), gather(embed_cotangent)
    input_all, target_all = gather(input_ids), gather(target_ids)
    rows_here = embedding.shape[0]
    partial_value = lax.dot_general(gathered, embedding, (((1,), (1,)), ((), ())), preferred_element_type=f32)
    first_row = lax.axis_index("vocab") * rows_here
    logits = lax.psum(partial_value, "tok")
    capped, exponent, target_hot, local_total, local_target = column_stats(logits, first_row, target_all)
    row_total, target_logit = lax.psum((local_total, local_target), "vocab")
    log_total = softcap + jnp.log(row_total)
    logit_grad = column_grad(capped, exponent, target_hot, row_total, log_total)
    loss_all = log_total - target_logit + zloss_weight * log_total * log_total
    local_count = input_ids.shape[0]
    token_loss = lax.dynamic_slice_in_dim(loss_all, lax.axis_index("vocab") * local_count, local_count, 0)
    hidden_grad = lax.psum_scatter(
        jnp.dot(logit_grad, embedding, preferred_element_type=f32), "vocab", scatter_dimension=0, tiled=True
    ).astype(bf16)
    columns = first_row + jnp.arange(rows_here, dtype=jnp.int32)
    input_hot = (input_all[:, None] == columns[None, :]).astype(bf16)
    head_grad = lax.dot_general(logit_grad, gathered, (((0,), (0,)), ((), ())), preferred_element_type=f32)
    inject = lax.dot_general(input_hot, cotangent, (((0,), (0,)), ((), ())), preferred_element_type=f32)
    embed_scale = math.sqrt(hidden.shape[1] * tok_count)
    embedding_grad = (head_grad + embed_scale * inject).astype(bf16)
    return (embedding_grad, hidden_grad, token_loss)


def dot(a, b, ca, cb):
    return lax.dot_general(a, b, (((ca,), (cb,)), ((), ())), preferred_element_type=f32)


def params(*names, vmem=None):
    return pltpu.CompilerParams(dimension_semantics=names, vmem_limit_bytes=vmem)


def cost(flops, nbytes, trans=0):
    return pl.CostEstimate(flops=flops, bytes_accessed=nbytes, transcendentals=trans)


def swap(x, bit, count):
    return lax.ppermute(x, "vocab", [(s, s ^ bit) for s in range(count)])


def swap_tok(x):
    return lax.ppermute(x, "tok", [(0, 1), (1, 0)])


def digits(ids):
    return [((ids >> shift) & 255).astype(bf16) for shift in (0, 8, 16)]


def undigits(columns):
    low, middle, high = (columns[:, k : k + 1].astype(f32).astype(jnp.int32) for k in range(3))
    return low + 256 * middle + 65536 * high


def side(base, far):
    return 1 - base[0] if far else base[0]


def tie(x, *others):
    return lax.optimization_barrier((x, *others))[0]


def merge_into(a0, a1, b0, b1, hid, half):
    quarter = a0.shape[0] // 2
    hid[: 2 * quarter, :half] = a0[:, :half]
    hid[2 * quarter :, :half] = a1[:, :half]
    hid[:quarter, half:] = b0[:quarter, :]
    hid[quarter : 2 * quarter, half:] = b1[:quarter, :]
    hid[2 * quarter : 3 * quarter, half:] = b0[quarter:, :]
    hid[3 * quarter :, half:] = b1[quarter:, :]


def first_kernel(base, a0, a1, b0, b1, emb, out, hid, target, inputs, *, half):
    @pl.when(pl.program_id(0) == 0)
    def _():
        merge_into(a0, a1, b0, b1, hid, half)
        size = a0.shape[0]
        for k, part in enumerate((a0, a1)):
            codes = part[:, half : half + 128]
            target[k * size : (k + 1) * size, :] = undigits(codes[:, 0:3])
            inputs[k * size : (k + 1) * size, :] = undigits(codes[:, 3:6])

    out[...] = dot(hid[...], emb[...], 1, 1)


def first_logits(base, pieces, embedding, count, block):
    _, width = embedding.shape
    tokens = 2 * pieces[0].shape[0]
    whole = lambda i, b: (0, 0)
    return pl.pallas_call(
        functools.partial(first_kernel, half=width // 2),
        grid_spec=pltpu.PrefetchScalarGridSpec(
            num_scalar_prefetch=1,
            grid=(count // block,),
            in_specs=[pl.BlockSpec(p.shape, whole) for p in pieces]
            + [pl.BlockSpec((block, width), lambda i, b: (side(b, True) * (count // block) + i, 0))],
            out_specs=[
                pl.BlockSpec((tokens, block), lambda i, b: (0, i)),
                pl.BlockSpec((tokens, width), whole),
                pl.BlockSpec((tokens, 1), whole),
                pl.BlockSpec((tokens, 1), whole),
            ],
        ),
        out_shape=[
            jax.ShapeDtypeStruct((tokens, count), f32),
            jax.ShapeDtypeStruct((tokens, width), bf16),
            jax.ShapeDtypeStruct((tokens, 1), jnp.int32),
            jax.ShapeDtypeStruct((tokens, 1), jnp.int32),
        ],
        compiler_params=params("arbitrary"),
        cost_estimate=cost(2 * tokens * width * count, 2 * width * count),
    )(base, *pieces, embedding)


def logits_kernel(base, hid, emb, other, target, bent_ref, stats_ref, total, picked, slope, *, block, rows):
    step = pl.program_id(0)

    @pl.when(step == 0)
    def _():
        total[...] = jnp.zeros_like(total)
        picked[...] = jnp.zeros_like(picked)
        slope[...] = jnp.zeros_like(slope)

    logits = dot(hid[...], emb[...], 1, 1) + other[...]
    ratio = jnp.tanh(logits * (1.0 / softcap))
    exponent = jnp.exp(softcap * ratio - softcap)
    here = target[...] - (base[1] * rows + base[0] * (rows // 2) + step * block)
    lane = lax.broadcasted_iota(jnp.int32, ratio.shape, 1)
    chosen = jnp.where(lane == here, ratio, 0.0)
    bent = exponent * (1.0 - ratio * ratio)
    bent_ref[...] = bent
    total[...] += sum(exponent[:, k : k + 128] for k in range(0, block, 128))
    picked[...] += sum(chosen[:, k : k + 128] for k in range(0, block, 128))
    slope[...] += sum(bent[:, k : k + 128] for k in range(0, block, 128))

    @pl.when(step == pl.num_programs(0) - 1)
    def _():
        stats_ref[...] = jnp.zeros_like(stats_ref)
        stats_ref[0:1, :] = jnp.sum(total[...].T, axis=0, keepdims=True)
        stats_ref[1:2, :] = jnp.sum(picked[...].T, axis=0, keepdims=True)
        stats_ref[2:3, :] = jnp.sum(slope[...].T, axis=0, keepdims=True)


def own_logits(base, hid, embedding, other, target, block):
    tokens, width = hid.shape
    count = other.shape[1]
    return pl.pallas_call(
        functools.partial(logits_kernel, block=block, rows=embedding.shape[0]),
        grid_spec=pltpu.PrefetchScalarGridSpec(
            num_scalar_prefetch=1,
            grid=(count // block,),
            in_specs=[
                pl.BlockSpec((tokens, width), lambda i, b: (0, 0)),
                pl.BlockSpec((block, width), lambda i, b: (b[0] * (count // block) + i, 0)),
                pl.BlockSpec((tokens, block), lambda i, b: (0, i)),
                pl.BlockSpec((tokens, 1), lambda i, b: (0, 0)),
            ],
            out_specs=[
                pl.BlockSpec((tokens, block), lambda i, b: (0, i)),
                pl.BlockSpec((8, tokens), lambda i, b: (0, 0)),
            ],
            scratch_shapes=[pltpu.VMEM((tokens, 128), f32) for _ in range(3)],
        ),
        out_shape=[jax.ShapeDtypeStruct((tokens, count), f32), jax.ShapeDtypeStruct((8, tokens), f32)],
        compiler_params=params("arbitrary"),
        cost_estimate=cost(2 * tokens * width * count, 2 * width * count),
    )(base, hid, embedding, other, target)


def hidden_kernel(base, near, far, emb, stats_ref, target, grad_ref, *rest, block, tiles, rows):
    left_keep, left_sent, right_keep, right_sent, total, column = rest
    step = pl.program_id(0)

    @pl.when(step == 0)
    def _():
        total[...] = jnp.zeros_like(total)
        stats = stats_ref[...].T
        row_total, ratio, slope = stats[:, 0:1], stats[:, 1:2], stats[:, 2:3]
        column[0] = (1.0 + 2.0 * zloss_weight * (softcap + jnp.log(row_total))) / row_total
        column[1] = 1.0 - ratio * ratio
        column[2] = 1.0 / sent_scale(row_total, ratio, slope)

    first = place_of(base, step, tiles) * block + base[1] * rows

    def add(bent):
        lane = lax.broadcasted_iota(jnp.int32, bent.shape, 1)
        hot = jnp.where(lane == target[...] - first, column[1], 0.0)
        grad = (column[0] * bent[...] - hot).astype(bf16)
        grad_ref[...] = grad
        total[...] += dot(grad, emb[...], 1, 0)

    pl.when(step < tiles)(lambda: add(near))
    pl.when(step >= tiles)(lambda: add(far))

    @pl.when(step == pl.num_programs(0) - 1)
    def _():
        inverse = column[2]
        half = left_keep.shape[1]
        quarter = left_keep.shape[0] // 2
        rows_of = [slice(k * quarter, (k + 1) * quarter) for k in range(4)]
        one, two = rows_of[:2]
        left, right = slice(0, half), slice(half, 2 * half)
        for ref, at, source, columns in (
            (left_keep, one, rows_of[0], left),
            (left_keep, two, rows_of[1], left),
            (left_sent, one, rows_of[2], left),
            (left_sent, two, rows_of[3], left),
            (right_keep, one, rows_of[0], right),
            (right_keep, two, rows_of[2], right),
            (right_sent, one, rows_of[1], right),
            (right_sent, two, rows_of[3], right),
        ):
            ref[at, :] = (total[source, columns] * inverse[source, :]).astype(ref.dtype)


def place_of(base, step, tiles):
    return jnp.where(step < tiles, base[0] * tiles + step, (1 - base[0]) * tiles + step - tiles)


def sent_scale(row_total, ratio, slope):
    weight = (1.0 + 2.0 * zloss_weight * (softcap + jnp.log(row_total))) / row_total
    return jnp.maximum(weight * slope + (1.0 - ratio * ratio), 1e-30) * (1.0 / 4096.0)


def hidden_sum(base, near, far, embedding, stats, target, block):
    tokens, count = near.shape
    rows, width = embedding.shape
    tiles = count // block
    shape = (tokens // 2, width // 2)
    whole = lambda i, b: (0, 0)
    return pl.pallas_call(
        functools.partial(hidden_kernel, block=block, tiles=tiles, rows=rows),
        grid_spec=pltpu.PrefetchScalarGridSpec(
            num_scalar_prefetch=1,
            grid=(2 * tiles,),
            in_specs=[
                pl.BlockSpec((tokens, block), lambda i, b: (0, jnp.minimum(i, tiles - 1))),
                pl.BlockSpec((tokens, block), lambda i, b: (0, jnp.maximum(i - tiles, 0))),
                pl.BlockSpec((block, width), lambda i, b: (place_of(b, i, tiles), 0)),
                pl.BlockSpec((8, tokens), whole),
                pl.BlockSpec((tokens, 1), whole),
            ],
            out_specs=[pl.BlockSpec((tokens, block), lambda i, b: (0, i))] + [pl.BlockSpec(shape, whole) for _ in range(4)],
            scratch_shapes=[pltpu.VMEM((tokens, width), f32), pltpu.VMEM((3, tokens, 1), f32)],
        ),
        out_shape=[jax.ShapeDtypeStruct((tokens, rows), bf16)] + [jax.ShapeDtypeStruct(shape, f32) for _ in range(4)],
        compiler_params=params("arbitrary"),
        cost_estimate=cost(2 * tokens * width * rows, 2 * width * rows),
    )(base, near, far, embedding, stats, target)


GROUP = 16


def embed_kernel(base, listed, bounds, grad, hid, cot_a, cot_b, ids, listed_col, *rest, block, scale, skip, tiles):
    out, mixed = rest[-2:]
    out[...] = dot(grad[...], hid[...], 0, 0).astype(bf16)
    tile = place_of(base, skip + pl.program_id(0), tiles)
    split = cot_a.shape[0]
    first, last = bounds[tile], bounds[tile + 1]

    def group(g, carry):
        at = first + g * GROUP
        hot = jnp.where(listed_col[pl.ds(at, GROUP), :] == ids[...], 1.0, 0.0).astype(bf16)
        mixed[...] = scale * (dot(hot[:, :split], cot_a[...], 1, 0) + dot(hot[:, split:], cot_b[...], 1, 0))

        def one(k, carry):
            row = listed[at + k] - tile * block
            start = pl.multiple_of((row // 16) * 16, 16)
            near_row = lax.broadcasted_iota(jnp.int32, (16, out.shape[1]), 0) == row - start
            add = jnp.where(near_row, mixed[pl.ds(k, 1), :], 0.0)
            out[pl.ds(start, 16), :] = (out[pl.ds(start, 16), :].astype(f32) + add).astype(bf16)
            return carry

        return lax.fori_loop(0, jnp.minimum(GROUP, last - at), one, carry)

    lax.fori_loop(0, (last - first + GROUP - 1) // GROUP, group, 0)


def embed_grad(base, listed, bounds, grad, skip, steps, hid, cot, ids, block, scale, start):
    tokens, width = hid.shape
    rows = grad.shape[1]
    tiles = rows // block // 2
    whole = lambda i, *s: (0, 0)
    column = listed[:, None]
    extra = [] if start is None else [start]
    return pl.pallas_call(
        functools.partial(embed_kernel, block=block, scale=scale, skip=skip, tiles=tiles),
        grid_spec=pltpu.PrefetchScalarGridSpec(
            num_scalar_prefetch=3,
            grid=(steps,),
            in_specs=[
                pl.BlockSpec((tokens, block), lambda i, *s: (0, skip + i)),
                pl.BlockSpec((tokens, width), whole),
                pl.BlockSpec((tokens // 2, width), whole),
                pl.BlockSpec((tokens // 2, width), whole),
                pl.BlockSpec((1, tokens), whole),
                pl.BlockSpec(column.shape, whole),
            ]
            + [pl.BlockSpec(memory_space=pl.ANY) for _ in extra],
            out_specs=pl.BlockSpec((block, width), lambda i, b, *s: (place_of(b, skip + i, tiles), 0)),
            scratch_shapes=[pltpu.VMEM((GROUP, width), f32)],
        ),
        out_shape=jax.ShapeDtypeStruct((rows, width), bf16),
        input_output_aliases={9: 0} if extra else {},
        compiler_params=params("arbitrary"),
        cost_estimate=cost(2 * tokens * width * block * steps, 2 * width * block * steps),
    )(base, listed, bounds, grad, hid, *cot, ids, column, *extra)


def flipped(x, span):
    lane = jnp.arange(x.shape[1], dtype=jnp.int32)
    return jnp.where((lane // span) % 2 == 0, jnp.roll(x, -span, 1), jnp.roll(x, span, 1))


def local_rows(ids, first_row, rows, block):
    at = ids - first_row
    count = at.shape[0]
    order = jnp.arange(count, dtype=jnp.int32)
    repeat = jnp.any((at[:, None] == at[None, :]) & (order[None, :] < order[:, None]), axis=1)
    lead = (at >= 0) & (at < rows) & ~repeat
    rank = jnp.sum((lead[None, :] & (at[None, :] < at[:, None])).astype(jnp.int32), axis=1)
    slots = jnp.arange(count + GROUP, dtype=jnp.int32)
    listed = jnp.sum(jnp.where(lead[None, :] & (rank[None, :] == slots[:, None]), at[None, :] + 1, 0), axis=1) - 1
    edges = block * jnp.arange(rows // block + 1, dtype=jnp.int32)
    bounds = jnp.sum((lead[None, :] & (at[None, :] < edges[:, None])).astype(jnp.int32), axis=1)
    return at, listed, bounds


def permuted(hidden, embedding, embed_cotangent, input_ids, target_ids, tok_count, vocab_count):
    rows, width = embedding.shape
    own_tokens = hidden.shape[0]
    tokens = own_tokens * vocab_count
    half, half_rows = width // 2, rows // 2
    block = 1024
    bits = [vocab_count >> (k + 1) for k in range(vocab_count.bit_length() - 1)]
    core, place = lax.axis_index("tok"), lax.axis_index("vocab")
    base = jnp.stack([core, place]).astype(jnp.int32)
    across = functools.partial(swap, count=vocab_count)

    def grow(x, bit):
        return jnp.concatenate([x, across(x, bit)], axis=0)

    coded = jnp.stack(digits(target_ids) + digits(input_ids), axis=1)
    coded = jnp.pad(coded, ((0, 0), (0, 128 - coded.shape[1])))
    value = jnp.concatenate([hidden[:, :half], coded, hidden[:, half:]], axis=1)
    for bit in bits[:-2]:
        value = grow(value, bit)
    left = grow(value[:, : half + 128], bits[-2])
    right = grow(value[:, half + 128 :], bits[-1])
    left_other = across(left, bits[-1])
    right_other = across(right, bits[-2])

    cot = embed_cotangent
    for bit in bits[:-1]:
        other = across(cot, bit)
        cot = jnp.concatenate([cot, other], axis=0)

    sent, hid, target, inputs = first_logits(base, (left, left_other, right, right_other), embedding, half_rows, block)
    got = swap_tok(sent)
    input_row, listed, bounds = local_rows(inputs[:, 0], place * rows, rows, block)
    target = tie(target, listed, bounds, input_row)
    near, stats = own_logits(base, hid, embedding, got, target, block)
    far = swap_tok(near)

    stats = stats + swap_tok(stats)
    for k, bit in enumerate(bits):
        other = across(stats, bit)
        stats = stats + flipped(other, own_tokens << k)
    own_log = softcap + jnp.log(stats[0, :own_tokens])
    token_loss = own_log - softcap * stats[1, :own_tokens] + zloss_weight * own_log * own_log
    cot = (cot, across(tie(cot, stats), bits[-1]))

    grad, left, left_sent, right, right_sent = hidden_sum(base, near, far, embedding, stats, target, block)

    def fold(keep, sent, bit):
        return keep + across(sent.astype(jnp.float16), bit).astype(f32)

    embed = functools.partial(
        embed_grad, hid=hid, cot=cot, ids=input_row[None, :], block=block, scale=math.sqrt(width * tok_count)
    )
    tiles = half_rows // block
    embedding_grad = embed(base, listed, bounds, grad, 0, tiles, start=None)
    left = fold(left, left_sent, bits[-1])
    right = fold(right, right_sent, bits[-2])
    embedding_grad = embed(base, listed, bounds, grad, tiles, tiles // 2, start=embedding_grad)
    size = tokens // 4
    left = fold(left[:size], left[size:], bits[-2])
    right = fold(right[:size], right[size:], bits[-1])
    embedding_grad = embed(
        base, listed, bounds, grad, tiles + tiles // 2, tiles - tiles // 2, start=embedding_grad
    )
    value = jnp.concatenate([left, right], axis=1)
    blocks = [value[k * own_tokens : (k + 1) * own_tokens] for k in range(4)]
    hidden_grad = blocks[0]
    for block_, bit in zip(blocks[1:], (bits[0], bits[1], bits[0] ^ bits[1])):
        hidden_grad = fold(hidden_grad, block_, bit)
    own = stats[:, :own_tokens]
    hidden_grad = (hidden_grad * sent_scale(own[0], own[1], own[2])[:, None]).astype(bf16)
    return (embedding_grad, hidden_grad, token_loss)


def solution(mesh):
    vocab_count, tok_count = mesh.shape["vocab"], mesh.shape["tok"]
    paired = tok_count == 2 and vocab_count == 16

    def local(hidden, embedding, embed_cotangent, input_ids, target_ids):
        rows, width = embedding.shape
        args = (hidden, embedding, embed_cotangent, input_ids, target_ids, tok_count)
        if not paired:
            return plain(*args)
        assert rows % 2048 == 0 and width % 256 == 0
        return permuted(*args, vocab_count)

    return jax.shard_map(
        local,
        mesh=mesh,
        in_specs=(P("vocab", "tok"), P("vocab", "tok"), P("vocab", "tok"), P("vocab"), P("vocab")),
        out_specs=(P("vocab", "tok"), P("vocab", "tok"), P("vocab")),
        check_vma=False,
    )
```

time: 355 us -> 182 us (0.51)
  matrix products: 114 us -> 0 us
  waiting for transfers between devices: 158 us -> 47.1 us
  Pallas kernels: 0 us -> 86.7 us
  blocking collectives: 55.7 us -> 0 us
  starting transfers between devices: 0.16 us -> 32.1 us
  between operations: 14.5 us -> 0.88 us
  local copies, waits for them, and re-layouts: 1.66 us -> 5.35 us
    dot_general x4 -> x0, matrix products: 114 us -> none  [the longest x1 34.7 us: local(): lax.dot_general(input_hot, cotangent, (((0,), (0,)), ((), ())), preferred...]
    pallas_call x0 -> x6, Pallas kernels: none -> 86.7 us  [the longest x3 35.2 us: embed_grad(): pl.pallas_call(functools.partial(embed_kernel, block=block, scale=scale,...]
    all_gather x2 -> x0, waiting for transfers between devices: 62.5 us -> none  [the longest x1 62.5 us: local(): lax.all_gather(hidden, 'vocab', axis=0, tiled=True)]
    reduce_scatter x1 -> x0, waiting for transfers between devices: 61.1 us -> none  [local(): lax.psum_scatter(jnp.dot(logit_grad, embedding, preferred_element_type=jn...]
    ppermute x0 -> x24, waiting for transfers between devices: none -> 47.1 us  [the longest x21 37.6 us: swap(): return lax.ppermute(x, 'vocab', [(s, s ^ bit) for s in range(count)])]
    psum x1 -> x0, blocking collectives: 42.4 us -> none  [local(): row_total, target_logit = lax.psum((local_total, local_target), 'vocab')]
    psum x1 -> x0, waiting for transfers between devices: 33.3 us -> none  [local(): logits = lax.psum(partial_value, 'tok')]
    ppermute x0 -> x24, starting transfers between devices: none -> 32.1 us  [the longest x21 31.8 us: swap(): return lax.ppermute(x, 'vocab', [(s, s ^ bit) for s in range(count)])]
  transfers between devices with their start and end apart: 4 -> 24, of which waited for: 3 -> 14; matrix products, arithmetic and copies ran while one was open for 29% -> 5% of each run, Pallas kernels for 0% -> 33%
where the time goes in v1:
time: 182 us; the launch traced here: 181 us
  Pallas kernels  86.7 us (48%)
  waiting for transfers between devices  47.1 us (26%)
  starting transfers between devices  32.1 us (18%)
  other arithmetic  8.91 us (5%)
  local copies, waits for them, and re-layouts  5.35 us (3%)
    ppermute x21, waiting for transfers between devices, swap(): return lax.ppermute(x, 'vocab', [(s, s ^ bit) for s in range(count)])  37.6 us
    pallas_call x3, Pallas kernels, embed_grad(): pl.pallas_call(functools.partial(embed_kernel, block=block, scale=scale,...  35.2 us
    ppermute x21, starting transfers between devices, swap(): return lax.ppermute(x, 'vocab', [(s, s ^ bit) for s in range(count)])  31.8 us
    pallas_call x1, Pallas kernels, hidden_sum(): pl.pallas_call(functools.partial(hidden_kernel, block=block, tiles=tiles,...  24.2 us
    pallas_call x1, Pallas kernels, own_logits(): pl.pallas_call(functools.partial(logits_kernel, block=block, rows=embeddi...  15 us
    pallas_call x1, Pallas kernels, first_logits(): pl.pallas_call(functools.partial(first_kernel, half=width // 2), grid_spe...  12.4 us
    ppermute x3, waiting for transfers between devices, swap_tok(): return lax.ppermute(x, 'tok', [(0, 1), (1, 0)])  9.49 us
  transfers between devices with their start and end apart: 24, of which 14 were waited for; matrix products, arithmetic and copies ran while one was open for 5% of the time, Pallas kernels for 33%

profile of v1, /device:TPU:0, one launch (start us, length us, event | category | flops | bytes accessed | tf_op | source)
XLA Modules:
  0.0 181.0 jit_solution(12875234193516115660)
XLA Ops:
  2.3 4.1 %collective-permute-start = (bf16[24,1920]{1,0:T(8,128)(2,1)S(1)}, bf16[24,1920]{1,0:T(8,128)(2,1)S(1)}, u32[]{:S(2)}, u32[]{:S(2)}) collective-permute-start(bf16[24,1920]{1,0:T(8,128)(2,1)S(1)} %pad_maximum_fusion.8), channel_id=1, source_target_pairs={{0,16},{2,18},{4,20},{6,22},{8,24},{10,26},{12,28},{14,30},{16,0},... | collective-permute-start | bytes 276488 | tf_op jit(solution)/shard_map/ppermute | solution.py:75
  6.4 4.6 %collective-permute-done = bf16[24,1920]{1,0:T(8,128)(2,1)S(1)} collective-permute-done((bf16[24,1920]{1,0:T(8,128)(2,1)S(1)}, bf16[24,1920]{1,0:T(8,128)(2,1)S(1)}, u32[]{:S(2)}, u32[]{:S(2)}) %collective-permute-start) | collective-permute-done | bytes 92192 | tf_op jit(solution)/shard_map/ppermute | solution.py:75
  11.9 4.8 %collective-permute-done.1 = bf16[48,1920]{1,0:T(8,128)(2,1)S(1)} collective-permute-done((bf16[48,1920]{1,0:T(8,128)(2,1)S(1)}, bf16[48,1920]{1,0:T(8,128)(2,1)S(1)}, u32[]{:S(2)}, u32[]{:S(2)}) %collective-permute-start.1) | collective-permute-done | bytes 184352 | tf_op jit(solution)/shard_map/ppermute | solution.py:75
  16.7 1.7 collective-permute-start.2
  18.4 1.6 collective-permute-start.4
  20.0 2.5 %collective-permute-done.2 = bf16[96,1024]{1,0:T(8,128)(2,1)S(1)} collective-permute-done((bf16[96,1024]{1,0:T(8,128)(2,1)S(1)}, bf16[96,1024]{1,0:T(8,128)(2,1)S(1)}, u32[]{:S(2)}, u32[]{:S(2)}) %collective-permute-start.2) | collective-permute-done | bytes 196640 | tf_op jit(solution)/shard_map/ppermute | solution.py:75
  22.5 1.6 collective-permute-start.3
  26.4 6.3 %collective-permute-done.5.b1 = bf16[192,896]{1,0:T(8,128)(2,1)S(1)} collective-permute-done((bf16[192,896]{1,0:T(8,128)(2,1)S(1)}, bf16[192,896]{1,0:T(8,128)(2,1)S(1)}, u32[]{:S(2)}, u32[]{:S(2)}) %collective-permute-start.5) | collective-permute-done | bytes 344096 | tf_op jit(solution)/shard_map/ppermute | solution.py:75
  34.3 12.4 %shard_map.76 = (f32[384,4096]{1,0:T(8,128)}, bf16[384,1792]{1,0:T(8,128)(2,1)}, s32[384,1]{1,0:T(8,128)}, s32[384,1]{1,0:T(8,128)}) custom-call(s32[2]{0:T(128)} %pad_add_fusion.base, bf16[192,1024]{1,0:T(8,128)(2,1)} %copy-done.2, bf16[192,1024]{1,0:T(8,128)(2,1)} %copy-done.7, bf16[192,896]{1,0:T(8,128)(2,1)} %copy-done.3, bf16[192,896]{1,0:T(8,128)(2,1)} %copy-done.8, ...), custom_call_target="tpu_custom_call" | custom-call | flops 5637144576 | bytes 14680064 | tf_op jit(solution)/shard_map/pallas_call | solution.py:126
  49.1 8.0 %collective-permute-done.6.other = f32[384,4096]{1,0:T(8,128)} collective-permute-done((f32[384,4096]{1,0:T(8,128)}, f32[384,4096]{1,0:T(8,128)}, u32[]{:S(2)}, u32[]{:S(2)}) %collective-permute-start.6) | collective-permute-done | bytes 6291488 | tf_op jit(solution)/shard_map/ppermute | solution.py:79
  57.1 15.0 %shard_map.77 = (f32[384,4096]{1,0:T(8,128)}, f32[8,384]{1,0:T(8,128)}) custom-call(s32[2]{0:T(128)} %pad_add_fusion.base, bf16[384,1792]{1,0:T(8,128)(2,1)} %get-tuple-element.17.hid, bf16[8192,1792]{1,0:T(8,128)(2,1)} %emb.5, f32[384,4096]{1,0:T(8,128)} %collective-permute-done.6.other, s32[384,1]{1,0:T(8,128)} %get-tuple-element.20.target), custom_call_target="tpu_custom_call" | custom-call | flops 5637144576 | bytes 14680064 | tf_op jit(solution)/shard_map/pallas_call | solution.py:183
  72.3 3.5 %collective-permute-start.13 = (bf16[24,1792]{1,0:T(8,128)(2,1)S(1)}, bf16[24,1792]{1,0:T(8,128)(2,1)S(1)}, u32[]{:S(2)}, u32[]{:S(2)}) collective-permute-start(bf16[24,1792]{1,0:T(8,128)(2,1)S(1)} %copy-done.4), channel_id=1, source_target_pairs={{0,16},{2,18},{4,20},{6,22},{8,24},{10,26},{12,28},{14,30},{16,0},... | collective-permute-start | bytes 258056 | tf_op jit(solution)/shard_map/ppermute | solution.py:75
  76.0 4.7 %collective-permute-done.13 = bf16[24,1792]{1,0:T(8,128)(2,1)S(1)} collective-permute-done((bf16[24,1792]{1,0:T(8,128)(2,1)S(1)}, bf16[24,1792]{1,0:T(8,128)(2,1)S(1)}, u32[]{:S(2)}, u32[]{:S(2)}) %collective-permute-start.13) | collective-permute-done | bytes 86048 | tf_op jit(solution)/shard_map/ppermute | solution.py:75
  83.4 3.5 %collective-permute-start.9 = (f32[8,384]{1,0:T(8,128)S(1)}, f32[8,384]{1,0:T(8,128)S(1)}, u32[]{:S(2)}, u32[]{:S(2)}) collective-permute-start(f32[8,384]{1,0:T(8,128)S(1)} %add.105), channel_id=1, source_target_pairs={{0,16},{2,18},{4,20},{6,22},{8,24},{10,26},{12,28},{14,30},{16,0},... | collective-permute-start | bytes 36872 | tf_op jit(solution)/shard_map/ppermute | solution.py:75
  86.9 1.7 collective-permute-done.9
  90.0 1.6 collective-permute-start.15
  94.2 5.1 %collective-permute-done.11 = f32[8,384]{1,0:T(8,128)S(1)} collective-permute-done((f32[8,384]{1,0:T(8,128)S(1)}, f32[8,384]{1,0:T(8,128)S(1)}, u32[]{:S(2)}, u32[]{:S(2)}) %collective-permute-start.11) | collective-permute-done | bytes 12320 | tf_op jit(solution)/shard_map/ppermute | solution.py:75
  105.1 24.2 %shard_map.78 = (bf16[384,8192]{1,0:T(8,128)(2,1)}, f32[192,896]{1,0:T(8,128)}, f32[192,896]{1,0:T(8,128)}, f32[192,896]{1,0:T(8,128)}, f32[192,896]{1,0:T(8,128)}) custom-call(s32[2]{0:T(128)} %pad_add_fusion.base, f32[384,4096]{1,0:T(8,128)} %get-tuple-element.21.near, f32[384,4096]{1,0:T(8,128)} %collective-permute-done.7.far, bf16[8192,1792]{1,0:T(8,128)(2,1)} %emb.5, ...), custom_call_target="tpu_custom_call" | custom-call | flops 11274289152 | bytes 29360128 | tf_op jit(solution)/shard_map/pallas_call | solution.py:267
  132.6 1.6 collective-permute-start.17
  135.0 15.2 %shard_map.79.rest_0_ = bf16[8192,1792]{1,0:T(8,128)(2,1)} custom-call(s32[2]{0:T(128)} %pad_add_fusion.base, s32[400]{0:T(512)} %copy-done.10, s32[9]{0:T(128)} %convert_reduce_fusion.1.bounds, bf16[384,8192]{1,0:T(8,128)(2,1)} %get-tuple-element.23.grad, bf16[384,1792]{1,0:T(8,128)(2,1)} %get-tuple-element.17.hid, bf16[192,1792]{1,0:T(8,128)(2,1)} %copy-done, ...), custom_call_target="tpu_custom_call" | custom-call | flops 5637144576 | bytes 14680064 | tf_op jit(solution)/shard_map/pallas_call | solution.py:323
  150.2 10.1 %shard_map.80.rest_0_ = bf16[8192,1792]{1,0:T(8,128)(2,1)} custom-call(s32[2]{0:T(128)} %pad_add_fusion.base, s32[400]{0:T(512)} %copy-done.10, s32[9]{0:T(128)} %convert_reduce_fusion.1.bounds, bf16[384,8192]{1,0:T(8,128)(2,1)} %get-tuple-element.23.grad, bf16[384,1792]{1,0:T(8,128)(2,1)} %get-tuple-element.17.hid, ...), custom_call_target="tpu_custom_call", output_to_operand_aliasing={{}: (9, {})} | custom-call | flops 2818572288 | bytes 7340032 | tf_op jit(solution)/shard_map/pallas_call | solution.py:323
  161.7 4.1 %collective-permute-done.20 = f16[96,896]{1,0:T(8,128)(2,1)S(1)} collective-permute-done((f16[96,896]{1,0:T(8,128)(2,1)S(1)}, f16[96,896]{1,0:T(8,128)(2,1)S(1)}, u32[]{:S(2)}, u32[]{:S(2)}) %collective-permute-start.20) | collective-permute-done | bytes 172064 | tf_op jit(solution)/shard_map/ppermute | solution.py:75
  166.2 2.7 %collective-permute-start.21 = (f16[24,1792]{1,0:T(8,128)(2,1)S(1)}, f16[24,1792]{1,0:T(8,128)(2,1)S(1)}, u32[]{:S(2)}, u32[]{:S(2)}) collective-permute-start(f16[24,1792]{1,0:T(8,128)(2,1)S(1)} %get-tuple-element.29), channel_id=1, source_target_pairs={{0,16},{2,18},{4,20},{6,22},{8,24},{10,26},{12,28},{14,30},{16,0},... | collective-permute-start | bytes 258056 | tf_op jit(solution)/shard_map/ppermute | solution.py:75
  170.4 9.9 %shard_map.81 = bf16[8192,1792]{1,0:T(8,128)(2,1)} custom-call(s32[2]{0:T(128)} %pad_add_fusion.base, s32[400]{0:T(512)} %copy-done.10, s32[9]{0:T(128)} %convert_reduce_fusion.1.bounds, bf16[384,8192]{1,0:T(8,128)(2,1)} %get-tuple-element.23.grad, bf16[384,1792]{1,0:T(8,128)(2,1)} %get-tuple-element.17.hid, ...), custom_call_target="tpu_custom_call", output_to_operand_aliasing={{}: (9, {})} | custom-call | flops 2818572288 | bytes 7340032 | tf_op jit(solution)/shard_map/pallas_call | solution.py:323
  (109 shorter events, 29.8 us)
Async XLA Ops:
  2.3 8.8 %collective-permute-start = (bf16[24,1920]{1,0:T(8,128)(2,1)S(1)}, bf16[24,1920]{1,0:T(8,128)(2,1)S(1)}, u32[]{:S(2)}, u32[]{:S(2)}) collective-permute-start(bf16[24,1920]{1,0:T(8,128)(2,1)S(1)} %pad_maximum_fusion.8), channel_id=1, source_target_pairs={{0,16},{2,18},{4,20},{6,22},{8,24},{10,26},{12,28},{14,30},{16,0},... | collective-permute-start | bytes 276488 | tf_op jit(solution)/shard_map/ppermute | solution.py:75
  11.1 5.6 %collective-permute-start.1 = (bf16[48,1920]{1,0:T(8,128)(2,1)S(1)}, bf16[48,1920]{1,0:T(8,128)(2,1)S(1)}, u32[]{:S(2)}, u32[]{:S(2)}) collective-permute-start(bf16[48,1920]{1,0:T(8,128)(2,1)S(1)} %pad_maximum_fusion.5), channel_id=1, source_target_pairs={{0,8},{2,10},{4,12},{6,14},{8,0},{10,2},{12,4},{14,6},{16,24},{18,... | collective-permute-start | bytes 552968 | tf_op jit(solution)/shard_map/ppermute | solution.py:75
  16.7 5.7 %collective-permute-start.2 = (bf16[96,1024]{1,0:T(8,128)(2,1)S(1)}, bf16[96,1024]{1,0:T(8,128)(2,1)S(1)}, u32[]{:S(2)}, u32[]{:S(2)}) collective-permute-start(bf16[96,1024]{1,0:T(8,128)(2,1)S(1)} %slice.145), channel_id=1, source_target_pairs={{0,4},{2,6},{4,0},{6,2},{8,12},{10,14},{12,8},{14,10},{16,20},{18,... | collective-permute-start | bytes 589832 | tf_op jit(solution)/shard_map/ppermute | solution.py:75
  18.4 7.0 %collective-permute-start.4 = (bf16[96,896]{1,0:T(8,128)(2,1)S(1)}, bf16[96,896]{1,0:T(8,128)(2,1)S(1)}, u32[]{:S(2)}, u32[]{:S(2)}) collective-permute-start(bf16[96,896]{1,0:T(8,128)(2,1)S(1)} %pad_maximum_fusion.6), channel_id=1, source_target_pairs={{0,2},{2,0},{4,6},{6,4},{8,10},{10,8},{12,14},{14,12},{16,18},{18,... | collective-permute-start | bytes 516104 | tf_op jit(solution)/shard_map/ppermute | solution.py:75
  22.5 10.3 %collective-permute-start.3 = (bf16[192,1024]{1,0:T(8,128)(2,1)S(1)}, bf16[192,1024]{1,0:T(8,128)(2,1)S(1)}, u32[]{:S(2)}, u32[]{:S(2)}) collective-permute-start(bf16[192,1024]{1,0:T(8,128)(2,1)S(1)} %pad_maximum_fusion.1.a0), channel_id=1, source_target_pairs={{0,2},{2,0},{4,6},{6,4},{8,10},{10,8},{12,14},{14,12},{16,18},{18,... | collective-permute-start | bytes 1179656 | tf_op jit(solution)/shard_map/ppermute | solution.py:75
  25.5 7.3 %collective-permute-start.5 = (bf16[192,896]{1,0:T(8,128)(2,1)S(1)}, bf16[192,896]{1,0:T(8,128)(2,1)S(1)}, u32[]{:S(2)}, u32[]{:S(2)}) collective-permute-start(bf16[192,896]{1,0:T(8,128)(2,1)S(1)} %pad_maximum_fusion.3.b0), channel_id=1, source_target_pairs={{0,4},{2,6},{4,0},{6,2},{8,12},{10,14},{12,8},{14,10},{16,20},{18,... | collective-permute-start | bytes 1032200 | tf_op jit(solution)/shard_map/ppermute | solution.py:75
  46.6 10.5 %collective-permute-start.6 = (f32[384,4096]{1,0:T(8,128)}, f32[384,4096]{1,0:T(8,128)}, u32[]{:S(2)}, u32[]{:S(2)}) collective-permute-start(f32[384,4096]{1,0:T(8,128)} %get-tuple-element.18), channel_id=1, source_target_pairs={{0,1},{1,0},{2,3},{3,2},{4,5},{5,4},{6,7},{7,6},{8,9},{9,8},{10,11... | collective-permute-start | bytes 18874376 | tf_op jit(solution)/shard_map/ppermute | solution.py:79
  72.2 32.9 %collective-permute-start.7 = (f32[384,4096]{1,0:T(8,128)}, f32[384,4096]{1,0:T(8,128)}, u32[]{:S(2)}, u32[]{:S(2)}) collective-permute-start(f32[384,4096]{1,0:T(8,128)} %get-tuple-element.21.near), channel_id=1, source_target_pairs={{0,1},{1,0},{2,3},{3,2},{4,5},{5,4},{6,7},{7,6},{8,9},{9,8},{10,11... | collective-permute-start | bytes 18874376 | tf_op jit(solution)/shard_map/ppermute | solution.py:79
  72.3 8.4 %collective-permute-start.13 = (bf16[24,1792]{1,0:T(8,128)(2,1)S(1)}, bf16[24,1792]{1,0:T(8,128)(2,1)S(1)}, u32[]{:S(2)}, u32[]{:S(2)}) collective-permute-start(bf16[24,1792]{1,0:T(8,128)(2,1)S(1)} %copy-done.4), channel_id=1, source_target_pairs={{0,16},{2,18},{4,20},{6,22},{8,24},{10,26},{12,28},{14,30},{16,0},... | collective-permute-start | bytes 258056 | tf_op jit(solution)/shard_map/ppermute | solution.py:75
  75.9 6.8 %collective-permute-start.8 = (f32[8,384]{1,0:T(8,128)}, f32[8,384]{1,0:T(8,128)S(1)}, u32[]{:S(2)}, u32[]{:S(2)}) collective-permute-start(f32[8,384]{1,0:T(8,128)} %get-tuple-element.22), channel_id=1, source_target_pairs={{0,1},{1,0},{2,3},{3,2},{4,5},{5,4},{6,7},{7,6},{8,9},{9,8},{10,11... | collective-permute-start | bytes 36872 | tf_op jit(solution)/shard_map/ppermute | solution.py:79
  80.7 9.2 %collective-permute-start.14 = (bf16[48,1792]{1,0:T(8,128)(2,1)S(1)}, bf16[48,1792]{1,0:T(8,128)(2,1)S(1)}, u32[]{:S(2)}, u32[]{:S(2)}) collective-permute-start(bf16[48,1792]{1,0:T(8,128)(2,1)S(1)} %pad_maximum_fusion.7), channel_id=1, source_target_pairs={{0,8},{2,10},{4,12},{6,14},{8,0},{10,2},{12,4},{14,6},{16,24},{18,... | collective-permute-start | bytes 516104 | tf_op jit(solution)/shard_map/ppermute | solution.py:75
  83.4 5.2 %collective-permute-start.9 = (f32[8,384]{1,0:T(8,128)S(1)}, f32[8,384]{1,0:T(8,128)S(1)}, u32[]{:S(2)}, u32[]{:S(2)}) collective-permute-start(f32[8,384]{1,0:T(8,128)S(1)} %add.105), channel_id=1, source_target_pairs={{0,16},{2,18},{4,20},{6,22},{8,24},{10,26},{12,28},{14,30},{16,0},... | collective-permute-start | bytes 36872 | tf_op jit(solution)/shard_map/ppermute | solution.py:75
  88.8 3.7 %collective-permute-start.10 = (f32[8,384]{1,0:T(8,128)S(1)}, f32[8,384]{1,0:T(8,128)S(1)}, u32[]{:S(2)}, u32[]{:S(2)}) collective-permute-start(f32[8,384]{1,0:T(8,128)S(1)} %fusion.10), channel_id=1, source_target_pairs={{0,8},{2,10},{4,12},{6,14},{8,0},{10,2},{12,4},{14,6},{16,24},{18,... | collective-permute-start | bytes 36872 | tf_op jit(solution)/shard_map/ppermute | solution.py:75
  90.0 10.6 %collective-permute-start.15 = (bf16[96,1792]{1,0:T(8,128)(2,1)S(1)}, bf16[96,1792]{1,0:T(8,128)(2,1)S(1)}, u32[]{:S(2)}, u32[]{:S(2)}) collective-permute-start(bf16[96,1792]{1,0:T(8,128)(2,1)S(1)} %pad_maximum_fusion.4), channel_id=1, source_target_pairs={{0,4},{2,6},{4,0},{6,2},{8,12},{10,14},{12,8},{14,10},{16,20},{18,... | collective-permute-start | bytes 1032200 | tf_op jit(solution)/shard_map/ppermute | solution.py:75
  92.7 6.6 %collective-permute-start.11 = (f32[8,384]{1,0:T(8,128)S(1)}, f32[8,384]{1,0:T(8,128)S(1)}, u32[]{:S(2)}, u32[]{:S(2)}) collective-permute-start(f32[8,384]{1,0:T(8,128)S(1)} %fusion.11), channel_id=1, source_target_pairs={{0,4},{2,6},{4,0},{6,2},{8,12},{10,14},{12,8},{14,10},{16,20},{18,... | collective-permute-start | bytes 36872 | tf_op jit(solution)/shard_map/ppermute | solution.py:75
  99.5 3.8 %collective-permute-start.12 = (f32[8,384]{1,0:T(8,128)S(1)}, f32[8,384]{1,0:T(8,128)S(1)}, u32[]{:S(2)}, u32[]{:S(2)}) collective-permute-start(f32[8,384]{1,0:T(8,128)S(1)} %fusion.12), channel_id=1, source_target_pairs={{0,2},{2,0},{4,6},{6,4},{8,10},{10,8},{12,14},{14,12},{16,18},{18,... | collective-permute-start | bytes 36872 | tf_op jit(solution)/shard_map/ppermute | solution.py:75
  103.5 30.6 %collective-permute-start.16 = (bf16[192,1792]{1,0:T(8,128)(2,1)S(1)}, bf16[192,1792]{1,0:T(8,128)(2,1)S(1)}, u32[]{:S(2)}, u32[]{:S(2)}) collective-permute-start(bf16[192,1792]{1,0:T(8,128)(2,1)S(1)} %constant_dynamic-update-slice_fusion.cot_a), channel_id=1, source_target_pairs={{0,2},{2,0},{4,6},{6,4},{8,10},{10,8},{12,14},{14,12},{16,18},{18,... | collective-permute-start | bytes 2064392 | tf_op jit(solution)/shard_map/ppermute | solution.py:75
  131.6 28.7 %collective-permute-start.19 = (f16[192,896]{1,0:T(8,128)(2,1)S(1)}, f16[192,896]{1,0:T(8,128)(2,1)S(1)}, u32[]{:S(2)}, u32[]{:S(2)}) collective-permute-start(f16[192,896]{1,0:T(8,128)(2,1)S(1)} %convert_element_type.72), channel_id=1, source_target_pairs={{0,4},{2,6},{4,0},{6,2},{8,12},{10,14},{12,8},{14,10},{16,20},{18,... | collective-permute-start | bytes 1032200 | tf_op jit(solution)/shard_map/ppermute | solution.py:75
  132.6 27.9 %collective-permute-start.17 = (f16[192,896]{1,0:T(8,128)(2,1)S(1)}, f16[192,896]{1,0:T(8,128)(2,1)S(1)}, u32[]{:S(2)}, u32[]{:S(2)}) collective-permute-start(f16[192,896]{1,0:T(8,128)(2,1)S(1)} %convert_element_type.69), channel_id=1, source_target_pairs={{0,2},{2,0},{4,6},{6,4},{8,10},{10,8},{12,14},{14,12},{16,18},{18,... | collective-permute-start | bytes 1032200 | tf_op jit(solution)/shard_map/ppermute | solution.py:75
  160.4 5.5 %collective-permute-start.20 = (f16[96,896]{1,0:T(8,128)(2,1)S(1)}, f16[96,896]{1,0:T(8,128)(2,1)S(1)}, u32[]{:S(2)}, u32[]{:S(2)}) collective-permute-start(f16[96,896]{1,0:T(8,128)(2,1)S(1)} %slice_convert_fusion), channel_id=1, source_target_pairs={{0,2},{2,0},{4,6},{6,4},{8,10},{10,8},{12,14},{14,12},{16,18},{18,... | collective-permute-start | bytes 516104 | tf_op jit(solution)/shard_map/ppermute | solution.py:75
  160.6 5.5 %collective-permute-start.18 = (f16[96,896]{1,0:T(8,128)(2,1)S(1)}, f16[96,896]{1,0:T(8,128)(2,1)S(1)}, u32[]{:S(2)}, u32[]{:S(2)}) collective-permute-start(f16[96,896]{1,0:T(8,128)(2,1)S(1)} %slice_convert_fusion.1), channel_id=1, source_target_pairs={{0,4},{2,6},{4,0},{6,2},{8,12},{10,14},{12,8},{14,10},{16,20},{18,... | collective-permute-start | bytes 516104 | tf_op jit(solution)/shard_map/ppermute | solution.py:75
  166.2 14.0 %collective-permute-start.21 = (f16[24,1792]{1,0:T(8,128)(2,1)S(1)}, f16[24,1792]{1,0:T(8,128)(2,1)S(1)}, u32[]{:S(2)}, u32[]{:S(2)}) collective-permute-start(f16[24,1792]{1,0:T(8,128)(2,1)S(1)} %get-tuple-element.29), channel_id=1, source_target_pairs={{0,16},{2,18},{4,20},{6,22},{8,24},{10,26},{12,28},{14,30},{16,0},... | collective-permute-start | bytes 258056 | tf_op jit(solution)/shard_map/ppermute | solution.py:75
  168.9 11.4 %collective-permute-start.23 = (f16[24,1792]{1,0:T(8,128)(2,1)S(1)}, f16[24,1792]{1,0:T(8,128)(2,1)S(1)}, u32[]{:S(2)}, u32[]{:S(2)}) collective-permute-start(f16[24,1792]{1,0:T(8,128)(2,1)S(1)} %get-tuple-element.30), channel_id=1, source_target_pairs={{0,24},{2,26},{4,28},{6,30},{8,16},{10,18},{12,20},{14,22},{16,8},... | collective-permute-start | bytes 258056 | tf_op jit(solution)/shard_map/ppermute | solution.py:75
  169.9 10.4 %collective-permute-start.22 = (f16[24,1792]{1,0:T(8,128)(2,1)S(1)}, f16[24,1792]{1,0:T(8,128)(2,1)S(1)}, u32[]{:S(2)}, u32[]{:S(2)}) collective-permute-start(f16[24,1792]{1,0:T(8,128)(2,1)S(1)} %get-tuple-element.31), channel_id=1, source_target_pairs={{0,8},{2,10},{4,12},{6,14},{8,0},{10,2},{12,4},{14,6},{16,24},{18,... | collective-permute-start | bytes 258056 | tf_op jit(solution)/shard_map/ppermute | solution.py:75
  (11 other events, 137.9 us)

commit v2 on v1

--- a/solution.py
+++ b/solution.py
@@ -13,6 +13,7 @@
 zloss_weight = 0.001
 f32 = jnp.float32
 bf16 = jnp.bfloat16
+f16 = jnp.float16
 
 
 def column_stats(logits, first_column, targets):
@@ -63,8 +64,8 @@
     return lax.dot_general(a, b, (((ca,), (cb,)), ((), ())), preferred_element_type=f32)
 
 
-def params(*names, vmem=None):
-    return pltpu.CompilerParams(dimension_semantics=names, vmem_limit_bytes=vmem)
+def params(mebibytes):
+    return pltpu.CompilerParams(dimension_semantics=("arbitrary",), vmem_limit_bytes=mebibytes << 20)
 
 
 def cost(flops, nbytes, trans=0):
@@ -143,7 +144,7 @@
             jax.ShapeDtypeStruct((tokens, 1), jnp.int32),
             jax.ShapeDtypeStruct((tokens, 1), jnp.int32),
         ],
-        compiler_params=params("arbitrary"),
+        compiler_params=params(28),
         cost_estimate=cost(2 * tokens * width * count, 2 * width * count),
     )(base, *pieces, embedding)
 
@@ -198,13 +199,13 @@
             scratch_shapes=[pltpu.VMEM((tokens, 128), f32) for _ in range(3)],
         ),
         out_shape=[jax.ShapeDtypeStruct((tokens, count), f32), jax.ShapeDtypeStruct((8, tokens), f32)],
-        compiler_params=params("arbitrary"),
+        compiler_params=params(30),
         cost_estimate=cost(2 * tokens * width * count, 2 * width * count),
     )(base, hid, embedding, other, target)
 
 
 def hidden_kernel(base, near, far, emb, stats_ref, target, grad_ref, *rest, block, tiles, rows):
-    left_keep, left_sent, right_keep, right_sent, total, column = rest
+    keep, sent, total, column = rest
     step = pl.program_id(0)
 
     @pl.when(step == 0)
@@ -230,23 +231,9 @@
 
     @pl.when(step == pl.num_programs(0) - 1)
     def _():
-        inverse = column[2]
-        half = left_keep.shape[1]
-        quarter = left_keep.shape[0] // 2
-        rows_of = [slice(k * quarter, (k + 1) * quarter) for k in range(4)]
-        one, two = rows_of[:2]
-        left, right = slice(0, half), slice(half, 2 * half)
-        for ref, at, source, columns in (
-            (left_keep, one, rows_of[0], left),
-            (left_keep, two, rows_of[1], left),
-            (left_sent, one, rows_of[2], left),
-            (left_sent, two, rows_of[3], left),
-            (right_keep, one, rows_of[0], right),
-            (right_keep, two, rows_of[2], right),
-            (right_sent, one, rows_of[1], right),
-            (right_sent, two, rows_of[3], right),
-        ):
-            ref[at, :] = (total[source, columns] * inverse[source, :]).astype(ref.dtype)
+        size = keep.shape[0]
+        keep[...] = total[:size, :] * column[2][:size]
+        sent[...] = total[size:, :] * column[2][size:]
 
 
 def place_of(base, step, tiles):
@@ -262,7 +249,7 @@
     tokens, count = near.shape
     rows, width = embedding.shape
     tiles = count // block
-    shape = (tokens // 2, width // 2)
+    shape = (tokens // 2, width)
     whole = lambda i, b: (0, 0)
     return pl.pallas_call(
         functools.partial(hidden_kernel, block=block, tiles=tiles, rows=rows),
@@ -276,52 +263,57 @@
                 pl.BlockSpec((8, tokens), whole),
                 pl.BlockSpec((tokens, 1), whole),
             ],
-            out_specs=[pl.BlockSpec((tokens, block), lambda i, b: (0, i))] + [pl.BlockSpec(shape, whole) for _ in range(4)],
+            out_specs=[pl.BlockSpec((tokens, block), lambda i, b: (0, i))] + [pl.BlockSpec(shape, whole) for _ in range(2)],
             scratch_shapes=[pltpu.VMEM((tokens, width), f32), pltpu.VMEM((3, tokens, 1), f32)],
         ),
-        out_shape=[jax.ShapeDtypeStruct((tokens, rows), bf16)] + [jax.ShapeDtypeStruct(shape, f32) for _ in range(4)],
-        compiler_params=params("arbitrary"),
+        out_shape=[jax.ShapeDtypeStruct((tokens, rows), bf16)] + [jax.ShapeDtypeStruct(shape, t) for t in (f32, f32)],
+        compiler_params=params(46),
         cost_estimate=cost(2 * tokens * width * rows, 2 * width * rows),
     )(base, near, far, embedding, stats, target)
 
 
-GROUP = 16
-
-
-def embed_kernel(base, listed, bounds, grad, hid, cot_a, cot_b, ids, listed_col, *rest, block, scale, skip, tiles):
+GROUP = 64
+
+
+def embed_kernel(base, listed, bounds, grad, hid, cot_a, cot_b, ids, listed_col, *rest, block, scale, skip, steps, tiles):
     out, mixed = rest[-2:]
     out[...] = dot(grad[...], hid[...], 0, 0).astype(bf16)
     tile = place_of(base, skip + pl.program_id(0), tiles)
     split = cot_a.shape[0]
-    first, last = bounds[tile], bounds[tile + 1]
-
-    def group(g, carry):
-        at = first + g * GROUP
-        hot = jnp.where(listed_col[pl.ds(at, GROUP), :] == ids[...], 1.0, 0.0).astype(bf16)
-        mixed[...] = scale * (dot(hot[:, :split], cot_a[...], 1, 0) + dot(hot[:, split:], cot_b[...], 1, 0))
-
-        def one(k, carry):
-            row = listed[at + k] - tile * block
-            start = pl.multiple_of((row // 16) * 16, 16)
-            near_row = lax.broadcasted_iota(jnp.int32, (16, out.shape[1]), 0) == row - start
-            add = jnp.where(near_row, mixed[pl.ds(k, 1), :], 0.0)
-            out[pl.ds(start, 16), :] = (out[pl.ds(start, 16), :].astype(f32) + add).astype(bf16)
+
+    opening = bounds[place_of(base, skip, tiles)]
+    ending = bounds[place_of(base, skip + steps - 1, tiles) + 1]
+
+    @pl.when(pl.program_id(0) == 0)
+    def _():
+        def group(g, carry):
+            at = pl.multiple_of(g * GROUP, GROUP)
+            hot = jnp.where(listed_col[pl.ds(opening + at, GROUP), :] == ids[...], 1.0, 0.0).astype(bf16)
+            rows = dot(hot[:, :split], cot_a[...], 1, 0) + dot(hot[:, split:], cot_b[...], 1, 0)
+            mixed[pl.ds(at, GROUP), :] = scale * rows
             return carry
 
-        return lax.fori_loop(0, jnp.minimum(GROUP, last - at), one, carry)
-
-    lax.fori_loop(0, (last - first + GROUP - 1) // GROUP, group, 0)
-
-
-def embed_grad(base, listed, bounds, grad, skip, steps, hid, cot, ids, block, scale, start):
+        lax.fori_loop(0, (ending - opening + GROUP - 1) // GROUP, group, 0)
+
+    def one(k, carry):
+        row = listed[k] - tile * block
+        start = pl.multiple_of((row // 16) * 16, 16)
+        near_row = lax.broadcasted_iota(jnp.int32, (16, out.shape[1]), 0) == row - start
+        add = jnp.where(near_row, mixed[pl.ds(k - opening, 1), :], 0.0)
+        out[pl.ds(start, 16), :] = (out[pl.ds(start, 16), :].astype(f32) + add).astype(bf16)
+        return carry
+
+    lax.fori_loop(bounds[tile], bounds[tile + 1], one, 0)
+
+
+def embed_grad(base, listed, bounds, grad, skip, steps, hid, cot, ids, column, block, scale, start):
     tokens, width = hid.shape
     rows = grad.shape[1]
     tiles = rows // block // 2
     whole = lambda i, *s: (0, 0)
-    column = listed[:, None]
     extra = [] if start is None else [start]
     return pl.pallas_call(
-        functools.partial(embed_kernel, block=block, scale=scale, skip=skip, tiles=tiles),
+        functools.partial(embed_kernel, block=block, scale=scale, skip=skip, steps=steps, tiles=tiles),
         grid_spec=pltpu.PrefetchScalarGridSpec(
             num_scalar_prefetch=3,
             grid=(steps,),
@@ -335,11 +327,11 @@
             ]
             + [pl.BlockSpec(memory_space=pl.ANY) for _ in extra],
             out_specs=pl.BlockSpec((block, width), lambda i, b, *s: (place_of(b, skip + i, tiles), 0)),
-            scratch_shapes=[pltpu.VMEM((GROUP, width), f32)],
+            scratch_shapes=[pltpu.VMEM((-(-tokens // GROUP) * GROUP, width), f32)],
         ),
         out_shape=jax.ShapeDtypeStruct((rows, width), bf16),
         input_output_aliases={9: 0} if extra else {},
-        compiler_params=params("arbitrary"),
+        compiler_params=params(50),
         cost_estimate=cost(2 * tokens * width * block * steps, 2 * width * block * steps),
     )(base, listed, bounds, grad, hid, *cot, ids, column, *extra)
 
@@ -360,7 +352,7 @@
     listed = jnp.sum(jnp.where(lead[None, :] & (rank[None, :] == slots[:, None]), at[None, :] + 1, 0), axis=1) - 1
     edges = block * jnp.arange(rows // block + 1, dtype=jnp.int32)
     bounds = jnp.sum((lead[None, :] & (at[None, :] < edges[:, None])).astype(jnp.int32), axis=1)
-    return at, listed, bounds
+    return at[None, :], listed, listed[:, None], bounds
 
 
 def permuted(hidden, embedding, embed_cotangent, input_ids, target_ids, tok_count, vocab_count):
@@ -394,8 +386,8 @@
 
     sent, hid, target, inputs = first_logits(base, (left, left_other, right, right_other), embedding, half_rows, block)
     got = swap_tok(sent)
-    input_row, listed, bounds = local_rows(inputs[:, 0], place * rows, rows, block)
-    target = tie(target, listed, bounds, input_row)
+    ids, listed, column, bounds = local_rows(inputs[:, 0], place * rows, rows, block)
+    target, ids, listed, column, bounds = lax.optimization_barrier((target, ids, listed, column, bounds))
     near, stats = own_logits(base, hid, embedding, got, target, block)
     far = swap_tok(near)
 
@@ -407,26 +399,23 @@
     token_loss = own_log - softcap * stats[1, :own_tokens] + zloss_weight * own_log * own_log
     cot = (cot, across(tie(cot, stats), bits[-1]))
 
-    grad, left, left_sent, right, right_sent = hidden_sum(base, near, far, embedding, stats, target, block)
+    grad, value, sent = hidden_sum(base, near, far, embedding, stats, target, 2 * block)
 
     def fold(keep, sent, bit):
-        return keep + across(sent.astype(jnp.float16), bit).astype(f32)
+        return keep + across(sent.astype(f16), bit).astype(f32)
 
     embed = functools.partial(
-        embed_grad, hid=hid, cot=cot, ids=input_row[None, :], block=block, scale=math.sqrt(width * tok_count)
+        embed_grad, hid=hid, cot=cot, ids=ids, column=column, block=block, scale=math.sqrt(width * tok_count)
     )
     tiles = half_rows // block
     embedding_grad = embed(base, listed, bounds, grad, 0, tiles, start=None)
-    left = fold(left, left_sent, bits[-1])
-    right = fold(right, right_sent, bits[-2])
+    value = fold(value, sent, bits[-1])
     embedding_grad = embed(base, listed, bounds, grad, tiles, tiles // 2, start=embedding_grad)
     size = tokens // 4
-    left = fold(left[:size], left[size:], bits[-2])
-    right = fold(right[:size], right[size:], bits[-1])
+    value = fold(value[:size], value[size:], bits[-2])
     embedding_grad = embed(
         base, listed, bounds, grad, tiles + tiles // 2, tiles - tiles // 2, start=embedding_grad
     )
-    value = jnp.concatenate([left, right], axis=1)
     blocks = [value[k * own_tokens : (k + 1) * own_tokens] for k in range(4)]
     hidden_grad = blocks[0]
     for block_, bit in zip(blocks[1:], (bits[0], bits[1], bits[0] ^ bits[1])):

time: 182 us -> 185 us (1.016)
  waiting for transfers between devices: 47.1 us -> 65.7 us
  Pallas kernels: 86.7 us -> 76.6 us
    ppermute x21 -> x19, waiting for transfers between devices: 37.6 us -> 49.8 us  [swap(): return lax.ppermute(x, 'vocab', [(s, s ^ bit) for s in range(count)])]
    ppermute x3, waiting for transfers between devices: 9.49 us -> 15.9 us  [swap_tok(): return lax.ppermute(x, 'tok', [(0, 1), (1, 0)])]
    pallas_call x3, Pallas kernels: 35.2 us -> 30 us  [embed_grad(): pl.pallas_call(functools.partial(embed_kernel, block=block, scale=scale,...]
    pallas_call x1, Pallas kernels: 24.2 us -> 21.9 us  [hidden_sum(): pl.pallas_call(functools.partial(hidden_kernel, block=block, tiles=tiles,...]
    pallas_call x1, Pallas kernels: 15 us -> 12.8 us  [own_logits(): pl.pallas_call(functools.partial(logits_kernel, block=block, rows=embeddi...]
    ppermute x21 -> x19, starting transfers between devices: 31.8 us -> 30.2 us  [swap(): return lax.ppermute(x, 'vocab', [(s, s ^ bit) for s in range(count)])]
  transfers between devices with their start and end apart: 24 -> 22, of which waited for: 14 -> 13; matrix products, arithmetic and copies ran while one was open for 5% -> 3% of each run, Pallas kernels for 33% -> 28%
where the time goes in v2:
time: 185 us
  Pallas kernels  76.6 us (41%)
  waiting for transfers between devices  65.7 us (36%)
  starting transfers between devices  30.5 us (16%)
  other arithmetic  7.12 us (4%)
  local copies, waits for them, and re-layouts  4.33 us (2%)
    ppermute x19, waiting for transfers between devices, swap(): return lax.ppermute(x, 'vocab', [(s, s ^ bit) for s in range(count)])  49.8 us
    ppermute x19, starting transfers between devices, swap(): return lax.ppermute(x, 'vocab', [(s, s ^ bit) for s in range(count)])  30.2 us
    pallas_call x3, Pallas kernels, embed_grad(): pl.pallas_call(functools.partial(embed_kernel, block=block, scale=scale,...  30 us
    pallas_call x1, Pallas kernels, hidden_sum(): pl.pallas_call(functools.partial(hidden_kernel, block=block, tiles=tiles,...  21.9 us
    ppermute x3, waiting for transfers between devices, swap_tok(): return lax.ppermute(x, 'tok', [(0, 1), (1, 0)])  15.9 us
    pallas_call x1, Pallas kernels, own_logits(): pl.pallas_call(functools.partial(logits_kernel, block=block, rows=embeddi...  12.8 us
    pallas_call x1, Pallas kernels, first_logits(): pl.pallas_call(functools.partial(first_kernel, half=width // 2), grid_spe...  11.8 us
  transfers between devices with their start and end apart: 22, of which 13 were waited for; matrix products, arithmetic and copies ran while one was open for 3% of the time, Pallas kernels for 28%

profile of v2, /device:TPU:0, one launch (start us, length us, event | category | flops | bytes accessed | tf_op | source)
XLA Modules:
  0.0 184.9 jit_solution(16624617269421082523)
XLA Ops:
  2.3 4.1 %collective-permute-start = (bf16[24,1920]{1,0:T(8,128)(2,1)S(1)}, bf16[24,1920]{1,0:T(8,128)(2,1)S(1)}, u32[]{:S(2)}, u32[]{:S(2)}) collective-permute-start(bf16[24,1920]{1,0:T(8,128)(2,1)S(1)} %pad_maximum_fusion.7), channel_id=1, source_target_pairs={{0,16},{2,18},{4,20},{6,22},{8,24},{10,26},{12,28},{14,30},{16,0},... | collective-permute-start | bytes 276488 | tf_op jit(solution)/shard_map/ppermute | solution.py:76
  6.4 4.6 %collective-permute-done = bf16[24,1920]{1,0:T(8,128)(2,1)S(1)} collective-permute-done((bf16[24,1920]{1,0:T(8,128)(2,1)S(1)}, bf16[24,1920]{1,0:T(8,128)(2,1)S(1)}, u32[]{:S(2)}, u32[]{:S(2)}) %collective-permute-start) | collective-permute-done | bytes 92192 | tf_op jit(solution)/shard_map/ppermute | solution.py:76
  11.9 4.8 %collective-permute-done.1 = bf16[48,1920]{1,0:T(8,128)(2,1)S(1)} collective-permute-done((bf16[48,1920]{1,0:T(8,128)(2,1)S(1)}, bf16[48,1920]{1,0:T(8,128)(2,1)S(1)}, u32[]{:S(2)}, u32[]{:S(2)}) %collective-permute-start.1) | collective-permute-done | bytes 184352 | tf_op jit(solution)/shard_map/ppermute | solution.py:76
  16.7 1.7 collective-permute-start.2
  20.0 2.5 %collective-permute-done.2 = bf16[96,1024]{1,0:T(8,128)(2,1)S(1)} collective-permute-done((bf16[96,1024]{1,0:T(8,128)(2,1)S(1)}, bf16[96,1024]{1,0:T(8,128)(2,1)S(1)}, u32[]{:S(2)}, u32[]{:S(2)}) %collective-permute-start.2) | collective-permute-done | bytes 196640 | tf_op jit(solution)/shard_map/ppermute | solution.py:76
  25.8 7.0 %collective-permute-done.5.b1 = bf16[192,896]{1,0:T(8,128)(2,1)S(1)} collective-permute-done((bf16[192,896]{1,0:T(8,128)(2,1)S(1)}, bf16[192,896]{1,0:T(8,128)(2,1)S(1)}, u32[]{:S(2)}, u32[]{:S(2)}) %collective-permute-start.5) | collective-permute-done | bytes 344096 | tf_op jit(solution)/shard_map/ppermute | solution.py:76
  32.8 11.8 %shard_map.76 = (f32[384,4096]{1,0:T(8,128)}, bf16[384,1792]{1,0:T(8,128)(2,1)S(1)}, s32[384,1]{1,0:T(8,128)S(1)}, s32[384,1]{1,0:T(8,128)S(1)}) custom-call(s32[2]{0:T(128)S(1)} %pad_add_fusion.base, bf16[192,1024]{1,0:T(8,128)(2,1)S(1)} %pad_maximum_fusion.a0, bf16[192,1024]{1,0:T(8,128)(2,1)S(1)} %collective-permute-done.3.a1, ...), custom_call_target="tpu_custom_call" | custom-call | flops 5637144576 | bytes 14680064 | tf_op jit(solution)/shard_map/pallas_call | solution.py:127
  45.7 9.4 %collective-permute-done.6.other = f32[384,4096]{1,0:T(8,128)} collective-permute-done((f32[384,4096]{1,0:T(8,128)}, f32[384,4096]{1,0:T(8,128)}, u32[]{:S(2)}, u32[]{:S(2)}) %collective-permute-start.6) | collective-permute-done | bytes 6291488 | tf_op jit(solution)/shard_map/ppermute | solution.py:80
  55.1 12.8 %shard_map.77 = (f32[384,4096]{1,0:T(8,128)S(1)}, f32[8,384]{1,0:T(8,128)S(1)}) custom-call(s32[2]{0:T(128)S(1)} %pad_add_fusion.base, bf16[384,1792]{1,0:T(8,128)(2,1)S(1)} %get-tuple-element.22.hid, bf16[8192,1792]{1,0:T(8,128)(2,1)} %emb.5, f32[384,4096]{1,0:T(8,128)} %collective-permute-done.6.other, s32[384,1]{1,0:T(8,128)S(1)} %get-tuple-element.24.target), custom_call_target="tpu_custom_call" | custom-call | flops 5637144576 | bytes 14680064 | tf_op jit(solution)/shard_map/pallas_call | solution.py:184
  68.2 3.5 %collective-permute-start.13 = (bf16[24,1792]{1,0:T(8,128)(2,1)S(1)}, bf16[24,1792]{1,0:T(8,128)(2,1)S(1)}, u32[]{:S(2)}, u32[]{:S(2)}) collective-permute-start(bf16[24,1792]{1,0:T(8,128)(2,1)S(1)} %copy-done.3), channel_id=1, source_target_pairs={{0,16},{2,18},{4,20},{6,22},{8,24},{10,26},{12,28},{14,30},{16,0},... | collective-permute-start | bytes 258056 | tf_op jit(solution)/shard_map/ppermute | solution.py:76
  71.8 6.5 %collective-permute-done.8 = f32[8,384]{1,0:T(8,128)S(1)} collective-permute-done((f32[8,384]{1,0:T(8,128)S(1)}, f32[8,384]{1,0:T(8,128)S(1)}, u32[]{:S(2)}, u32[]{:S(2)}) %collective-permute-start.8) | collective-permute-done | bytes 12320 | tf_op jit(solution)/shard_map/ppermute | solution.py:80
  78.2 3.5 %collective-permute-start.9 = (f32[8,384]{1,0:T(8,128)S(1)}, f32[8,384]{1,0:T(8,128)S(1)}, u32[]{:S(2)}, u32[]{:S(2)}) collective-permute-start(f32[8,384]{1,0:T(8,128)S(1)} %add.99), channel_id=1, source_target_pairs={{0,16},{2,18},{4,20},{6,22},{8,24},{10,26},{12,28},{14,30},{16,0},... | collective-permute-start | bytes 36872 | tf_op jit(solution)/shard_map/ppermute | solution.py:76
  81.7 1.7 collective-permute-done.9
  84.8 2.5 %collective-permute-done.10 = f32[8,384]{1,0:T(8,128)S(1)} collective-permute-done((f32[8,384]{1,0:T(8,128)S(1)}, f32[8,384]{1,0:T(8,128)S(1)}, u32[]{:S(2)}, u32[]{:S(2)}) %collective-permute-start.10) | collective-permute-done | bytes 12320 | tf_op jit(solution)/shard_map/ppermute | solution.py:76
  92.7 1.9 %collective-permute-done.14 = bf16[48,1792]{1,0:T(8,128)(2,1)S(1)} collective-permute-done((bf16[48,1792]{1,0:T(8,128)(2,1)S(1)}, bf16[48,1792]{1,0:T(8,128)(2,1)S(1)}, u32[]{:S(2)}, u32[]{:S(2)}) %collective-permute-start.14) | collective-permute-done | bytes 172064 | tf_op jit(solution)/shard_map/ppermute | solution.py:76
  96.0 2.6 %copy-done.2 = f32[384,4096]{1,0:T(8,128)} copy-done((f32[384,4096]{1,0:T(8,128)}, f32[384,4096]{1,0:T(8,128)S(1)}, u32[]{:S(2)}) %copy-start.2) | copy-done | bytes 6291480
  98.6 21.9 %shard_map.78 = (bf16[384,8192]{1,0:T(8,128)(2,1)}, f32[192,1792]{1,0:T(8,128)S(1)}, f32[192,1792]{1,0:T(8,128)S(1)}) custom-call(s32[2]{0:T(128)S(1)} %pad_add_fusion.base, f32[384,4096]{1,0:T(8,128)} %copy-done, f32[384,4096]{1,0:T(8,128)} %copy-done.2, bf16[8192,1792]{1,0:T(8,128)(2,1)} %emb.5, f32[8,384]{1,0:T(8,128)S(1)} %maximum_add_fusion.stats_ref, ...), custom_call_target="tpu_custom_call" | custom-call | flops 11274289152 | bytes 29360128 | tf_op jit(solution)/shard_map/pallas_call | solution.py:254
  124.3 15.8 %collective-permute-done.17 = f16[192,1792]{1,0:T(8,128)(2,1)} collective-permute-done((f16[192,1792]{1,0:T(8,128)(2,1)}, f16[192,1792]{1,0:T(8,128)(2,1)}, u32[]{:S(2)}, u32[]{:S(2)}) %collective-permute-start.17) | collective-permute-done | bytes 688160 | tf_op jit(solution)/shard_map/ppermute | solution.py:76
  140.1 1.6 convert_add_fusion
  143.4 6.8 %collective-permute-done.16.cot_b = bf16[192,1792]{1,0:T(8,128)(2,1)S(1)} collective-permute-done((bf16[192,1792]{1,0:T(8,128)(2,1)S(1)}, bf16[192,1792]{1,0:T(8,128)(2,1)S(1)}, u32[]{:S(2)}, u32[]{:S(2)}) %collective-permute-start.16) | collective-permute-done | bytes 688160 | tf_op jit(solution)/shard_map/ppermute | solution.py:76
  150.2 13.1 %shard_map.79.rest_0_ = bf16[8192,1792]{1,0:T(8,128)(2,1)} custom-call(s32[2]{0:T(128)S(1)} %pad_add_fusion.base, s32[448]{0:T(512)S(1)} %broadcast_add_fusion.listed, s32[9]{0:T(128)S(1)} %convert_reduce_fusion.1.bounds, bf16[384,8192]{1,0:T(8,128)(2,1)} %get-tuple-element.27.grad, bf16[384,1792]{1,0:T(8,128)(2,1)S(1)} %get-tuple-element.22.hid, ...), custom_call_target="tpu_custom_call" | custom-call | flops 5637144576 | bytes 14680064 | tf_op jit(solution)/shard_map/pallas_call | solution.py:315
  163.3 8.4 %shard_map.80.rest_0_ = bf16[8192,1792]{1,0:T(8,128)(2,1)} custom-call(s32[2]{0:T(128)S(1)} %pad_add_fusion.base, s32[448]{0:T(512)S(1)} %broadcast_add_fusion.listed, s32[9]{0:T(128)S(1)} %convert_reduce_fusion.1.bounds, bf16[384,8192]{1,0:T(8,128)(2,1)} %get-tuple-element.27.grad, ...), custom_call_target="tpu_custom_call", output_to_operand_aliasing={{}: (9, {})} | custom-call | flops 2818572288 | bytes 7340032 | tf_op jit(solution)/shard_map/pallas_call | solution.py:315
  171.9 2.6 %collective-permute-start.19 = (f16[24,1792]{1,0:T(8,128)(2,1)S(1)}, f16[24,1792]{1,0:T(8,128)(2,1)S(1)}, u32[]{:S(2)}, u32[]{:S(2)}) collective-permute-start(f16[24,1792]{1,0:T(8,128)(2,1)S(1)} %get-tuple-element.35), channel_id=1, source_target_pairs={{0,16},{2,18},{4,20},{6,22},{8,24},{10,26},{12,28},{14,30},{16,0},... | collective-permute-start | bytes 258056 | tf_op jit(solution)/shard_map/ppermute | solution.py:76
  175.7 8.5 %shard_map.81 = bf16[8192,1792]{1,0:T(8,128)(2,1)} custom-call(s32[2]{0:T(128)S(1)} %pad_add_fusion.base, s32[448]{0:T(512)S(1)} %broadcast_add_fusion.listed, s32[9]{0:T(128)S(1)} %convert_reduce_fusion.1.bounds, bf16[384,8192]{1,0:T(8,128)(2,1)} %get-tuple-element.27.grad, ...), custom_call_target="tpu_custom_call", output_to_operand_aliasing={{}: (9, {})} | custom-call | flops 2818572288 | bytes 7340032 | tf_op jit(solution)/shard_map/pallas_call | solution.py:315
  (86 shorter events, 24.6 us)
Async XLA Ops:
  2.3 8.8 %collective-permute-start = (bf16[24,1920]{1,0:T(8,128)(2,1)S(1)}, bf16[24,1920]{1,0:T(8,128)(2,1)S(1)}, u32[]{:S(2)}, u32[]{:S(2)}) collective-permute-start(bf16[24,1920]{1,0:T(8,128)(2,1)S(1)} %pad_maximum_fusion.7), channel_id=1, source_target_pairs={{0,16},{2,18},{4,20},{6,22},{8,24},{10,26},{12,28},{14,30},{16,0},... | collective-permute-start | bytes 276488 | tf_op jit(solution)/shard_map/ppermute | solution.py:76
  11.1 5.6 %collective-permute-start.1 = (bf16[48,1920]{1,0:T(8,128)(2,1)S(1)}, bf16[48,1920]{1,0:T(8,128)(2,1)S(1)}, u32[]{:S(2)}, u32[]{:S(2)}) collective-permute-start(bf16[48,1920]{1,0:T(8,128)(2,1)S(1)} %pad_maximum_fusion.4), channel_id=1, source_target_pairs={{0,8},{2,10},{4,12},{6,14},{8,0},{10,2},{12,4},{14,6},{16,24},{18,... | collective-permute-start | bytes 552968 | tf_op jit(solution)/shard_map/ppermute | solution.py:76
  16.7 5.7 %collective-permute-start.2 = (bf16[96,1024]{1,0:T(8,128)(2,1)S(1)}, bf16[96,1024]{1,0:T(8,128)(2,1)S(1)}, u32[]{:S(2)}, u32[]{:S(2)}) collective-permute-start(bf16[96,1024]{1,0:T(8,128)(2,1)S(1)} %slice.136), channel_id=1, source_target_pairs={{0,4},{2,6},{4,0},{6,2},{8,12},{10,14},{12,8},{14,10},{16,20},{18,... | collective-permute-start | bytes 589832 | tf_op jit(solution)/shard_map/ppermute | solution.py:76
  18.4 7.0 %collective-permute-start.4 = (bf16[96,896]{1,0:T(8,128)(2,1)S(1)}, bf16[96,896]{1,0:T(8,128)(2,1)S(1)}, u32[]{:S(2)}, u32[]{:S(2)}) collective-permute-start(bf16[96,896]{1,0:T(8,128)(2,1)S(1)} %pad_maximum_fusion.5), channel_id=1, source_target_pairs={{0,2},{2,0},{4,6},{6,4},{8,10},{10,8},{12,14},{14,12},{16,18},{18,... | collective-permute-start | bytes 516104 | tf_op jit(solution)/shard_map/ppermute | solution.py:76
  22.5 10.3 %collective-permute-start.3 = (bf16[192,1024]{1,0:T(8,128)(2,1)S(1)}, bf16[192,1024]{1,0:T(8,128)(2,1)S(1)}, u32[]{:S(2)}, u32[]{:S(2)}) collective-permute-start(bf16[192,1024]{1,0:T(8,128)(2,1)S(1)} %pad_maximum_fusion.a0), channel_id=1, source_target_pairs={{0,2},{2,0},{4,6},{6,4},{8,10},{10,8},{12,14},{14,12},{16,18},{18,... | collective-permute-start | bytes 1179656 | tf_op jit(solution)/shard_map/ppermute | solution.py:76
  25.5 7.3 %collective-permute-start.5 = (bf16[192,896]{1,0:T(8,128)(2,1)S(1)}, bf16[192,896]{1,0:T(8,128)(2,1)S(1)}, u32[]{:S(2)}, u32[]{:S(2)}) collective-permute-start(bf16[192,896]{1,0:T(8,128)(2,1)S(1)} %pad_maximum_fusion.2.b0), channel_id=1, source_target_pairs={{0,4},{2,6},{4,0},{6,2},{8,12},{10,14},{12,8},{14,10},{16,20},{18,... | collective-permute-start | bytes 1032200 | tf_op jit(solution)/shard_map/ppermute | solution.py:76
  44.6 10.5 %collective-permute-start.6 = (f32[384,4096]{1,0:T(8,128)}, f32[384,4096]{1,0:T(8,128)}, u32[]{:S(2)}, u32[]{:S(2)}) collective-permute-start(f32[384,4096]{1,0:T(8,128)} %get-tuple-element.23), channel_id=1, source_target_pairs={{0,1},{1,0},{2,3},{3,2},{4,5},{5,4},{6,7},{7,6},{8,9},{9,8},{10,11... | collective-permute-start | bytes 18874376 | tf_op jit(solution)/shard_map/ppermute | solution.py:80
  55.1 13.1 %copy-start.3 = (bf16[24,1792]{1,0:T(8,128)(2,1)S(1)}, bf16[24,1792]{1,0:T(8,128)(2,1)}, u32[]{:S(2)}) copy-start(bf16[24,1792]{1,0:T(8,128)(2,1)} %param.7) | copy-start | bytes 258052
  68.0 28.0 %copy-start = (f32[384,4096]{1,0:T(8,128)}, f32[384,4096]{1,0:T(8,128)S(1)}, u32[]{:S(2)}) copy-start(f32[384,4096]{1,0:T(8,128)S(1)} %get-tuple-element.25.near) | copy-start | bytes 18874372
  68.0 28.0 %collective-permute-start.7 = (f32[384,4096]{1,0:T(8,128)S(1)}, f32[384,4096]{1,0:T(8,128)S(1)}, u32[]{:S(2)}, u32[]{:S(2)}) collective-permute-start(f32[384,4096]{1,0:T(8,128)S(1)} %get-tuple-element.25.near), channel_id=1, source_target_pairs={{0,1},{1,0},{2,3},{3,2},{4,5},{5,4},{6,7},{7,6},{8,9},{9,8},{10,11... | collective-permute-start | bytes 18874376 | tf_op jit(solution)/shard_map/ppermute | solution.py:80
  68.2 20.9 %collective-permute-start.13 = (bf16[24,1792]{1,0:T(8,128)(2,1)S(1)}, bf16[24,1792]{1,0:T(8,128)(2,1)S(1)}, u32[]{:S(2)}, u32[]{:S(2)}) collective-permute-start(bf16[24,1792]{1,0:T(8,128)(2,1)S(1)} %copy-done.3), channel_id=1, source_target_pairs={{0,16},{2,18},{4,20},{6,22},{8,24},{10,26},{12,28},{14,30},{16,0},... | collective-permute-start | bytes 258056 | tf_op jit(solution)/shard_map/ppermute | solution.py:76
  71.6 6.6 %collective-permute-start.8 = (f32[8,384]{1,0:T(8,128)S(1)}, f32[8,384]{1,0:T(8,128)S(1)}, u32[]{:S(2)}, u32[]{:S(2)}) collective-permute-start(f32[8,384]{1,0:T(8,128)S(1)} %get-tuple-element.26), channel_id=1, source_target_pairs={{0,1},{1,0},{2,3},{3,2},{4,5},{5,4},{6,7},{7,6},{8,9},{9,8},{10,11... | collective-permute-start | bytes 36872 | tf_op jit(solution)/shard_map/ppermute | solution.py:80
  78.2 5.1 %collective-permute-start.9 = (f32[8,384]{1,0:T(8,128)S(1)}, f32[8,384]{1,0:T(8,128)S(1)}, u32[]{:S(2)}, u32[]{:S(2)}) collective-permute-start(f32[8,384]{1,0:T(8,128)S(1)} %add.99), channel_id=1, source_target_pairs={{0,16},{2,18},{4,20},{6,22},{8,24},{10,26},{12,28},{14,30},{16,0},... | collective-permute-start | bytes 36872 | tf_op jit(solution)/shard_map/ppermute | solution.py:76
  83.6 3.7 %collective-permute-start.10 = (f32[8,384]{1,0:T(8,128)S(1)}, f32[8,384]{1,0:T(8,128)S(1)}, u32[]{:S(2)}, u32[]{:S(2)}) collective-permute-start(f32[8,384]{1,0:T(8,128)S(1)} %fusion.7), channel_id=1, source_target_pairs={{0,8},{2,10},{4,12},{6,14},{8,0},{10,2},{12,4},{14,6},{16,24},{18,... | collective-permute-start | bytes 36872 | tf_op jit(solution)/shard_map/ppermute | solution.py:76
  87.5 3.7 %collective-permute-start.11 = (f32[8,384]{1,0:T(8,128)S(1)}, f32[8,384]{1,0:T(8,128)S(1)}, u32[]{:S(2)}, u32[]{:S(2)}) collective-permute-start(f32[8,384]{1,0:T(8,128)S(1)} %fusion.8), channel_id=1, source_target_pairs={{0,4},{2,6},{4,0},{6,2},{8,12},{10,14},{12,8},{14,10},{16,20},{18,... | collective-permute-start | bytes 36872 | tf_op jit(solution)/shard_map/ppermute | solution.py:76
  89.1 5.5 %collective-permute-start.14 = (bf16[48,1792]{1,0:T(8,128)(2,1)S(1)}, bf16[48,1792]{1,0:T(8,128)(2,1)S(1)}, u32[]{:S(2)}, u32[]{:S(2)}) collective-permute-start(bf16[48,1792]{1,0:T(8,128)(2,1)S(1)} %pad_maximum_fusion.6), channel_id=1, source_target_pairs={{0,8},{2,10},{4,12},{6,14},{8,0},{10,2},{12,4},{14,6},{16,24},{18,... | collective-permute-start | bytes 516104 | tf_op jit(solution)/shard_map/ppermute | solution.py:76
  91.4 4.4 %collective-permute-start.12 = (f32[8,384]{1,0:T(8,128)S(1)}, f32[8,384]{1,0:T(8,128)S(1)}, u32[]{:S(2)}, u32[]{:S(2)}) collective-permute-start(f32[8,384]{1,0:T(8,128)S(1)} %fusion.9), channel_id=1, source_target_pairs={{0,2},{2,0},{4,6},{6,4},{8,10},{10,8},{12,14},{14,12},{16,18},{18,... | collective-permute-start | bytes 36872 | tf_op jit(solution)/shard_map/ppermute | solution.py:76
  95.3 27.4 %collective-permute-start.15 = (bf16[96,1792]{1,0:T(8,128)(2,1)}, bf16[96,1792]{1,0:T(8,128)(2,1)S(1)}, u32[]{:S(2)}, u32[]{:S(2)}) collective-permute-start(bf16[96,1792]{1,0:T(8,128)(2,1)} %pad_maximum_fusion.3), channel_id=1, source_target_pairs={{0,4},{2,6},{4,0},{6,2},{8,12},{10,14},{12,8},{14,10},{16,20},{18,... | collective-permute-start | bytes 1032200 | tf_op jit(solution)/shard_map/ppermute | solution.py:76
  121.5 18.6 %collective-permute-start.17 = (f16[192,1792]{1,0:T(8,128)(2,1)}, f16[192,1792]{1,0:T(8,128)(2,1)}, u32[]{:S(2)}, u32[]{:S(2)}) collective-permute-start(f16[192,1792]{1,0:T(8,128)(2,1)} %convert_element_type.59), channel_id=1, source_target_pairs={{0,2},{2,0},{4,6},{6,4},{8,10},{10,8},{12,14},{14,12},{16,18},{18,... | collective-permute-start | bytes 2064392 | tf_op jit(solution)/shard_map/ppermute | solution.py:76
  122.9 27.3 %collective-permute-start.16 = (bf16[192,1792]{1,0:T(8,128)(2,1)S(1)}, bf16[192,1792]{1,0:T(8,128)(2,1)S(1)}, u32[]{:S(2)}, u32[]{:S(2)}) collective-permute-start(bf16[192,1792]{1,0:T(8,128)(2,1)S(1)} %constant_dynamic-update-slice_fusion.cot_a), channel_id=1, source_target_pairs={{0,2},{2,0},{4,6},{6,4},{8,10},{10,8},{12,14},{14,12},{16,18},{18,... | collective-permute-start | bytes 2064392 | tf_op jit(solution)/shard_map/ppermute | solution.py:76
  141.8 29.9 %collective-permute-start.18 = (f16[96,1792]{1,0:T(8,128)(2,1)S(1)}, f16[96,1792]{1,0:T(8,128)(2,1)S(1)}, u32[]{:S(2)}, u32[]{:S(2)}) collective-permute-start(f16[96,1792]{1,0:T(8,128)(2,1)S(1)} %slice_convert_fusion), channel_id=1, source_target_pairs={{0,4},{2,6},{4,0},{6,2},{8,12},{10,14},{12,8},{14,10},{16,20},{18,... | collective-permute-start | bytes 1032200 | tf_op jit(solution)/shard_map/ppermute | solution.py:76
  171.9 12.4 %collective-permute-start.19 = (f16[24,1792]{1,0:T(8,128)(2,1)S(1)}, f16[24,1792]{1,0:T(8,128)(2,1)S(1)}, u32[]{:S(2)}, u32[]{:S(2)}) collective-permute-start(f16[24,1792]{1,0:T(8,128)(2,1)S(1)} %get-tuple-element.35), channel_id=1, source_target_pairs={{0,16},{2,18},{4,20},{6,22},{8,24},{10,26},{12,28},{14,30},{16,0},... | collective-permute-start | bytes 258056 | tf_op jit(solution)/shard_map/ppermute | solution.py:76
  174.4 9.8 %collective-permute-start.21 = (f16[24,1792]{1,0:T(8,128)(2,1)S(1)}, f16[24,1792]{1,0:T(8,128)(2,1)S(1)}, u32[]{:S(2)}, u32[]{:S(2)}) collective-permute-start(f16[24,1792]{1,0:T(8,128)(2,1)S(1)} %get-tuple-element.36), channel_id=1, source_target_pairs={{0,24},{2,26},{4,28},{6,30},{8,16},{10,18},{12,20},{14,22},{16,8},... | collective-permute-start | bytes 258056 | tf_op jit(solution)/shard_map/ppermute | solution.py:76
  175.5 8.7 %collective-permute-start.20 = (f16[24,1792]{1,0:T(8,128)(2,1)S(1)}, f16[24,1792]{1,0:T(8,128)(2,1)S(1)}, u32[]{:S(2)}, u32[]{:S(2)}) collective-permute-start(f16[24,1792]{1,0:T(8,128)(2,1)S(1)} %get-tuple-element.37), channel_id=1, source_target_pairs={{0,8},{2,10},{4,12},{6,14},{8,0},{10,2},{12,4},{14,6},{16,24},{18,... | collective-permute-start | bytes 258056 | tf_op jit(solution)/shard_map/ppermute | solution.py:76
  (2 other events, 4.9 us)
